TPU v7x, 512 devices: a 8x2x16 block of a 8x8x16 slice. The times are simulated.
512 devices in a mesh: groups: 2 (over y), date: 32 (over z, core), tile: 8 (over x).
Axes of the slice: x: 8, y: 2, z: 16, core: 2. Of those that a mesh axis runs over, the one named last changes fastest.
The devices are a block of a 8x8x16 slice.
Arguments:
- acquired: float32 [2, 256, 256, 128], P(None, 'date', ('groups', 'tile')), parts along dimension 2, may hold values from -10 to 10, as said below
Outputs:
- coherence: float32 [2, 4, 256, 8, 256, 128], P(None, None, 'date', None, ('groups', 'tile')), parts along dimension 4
There are 2 independent parts, one for each index of `groups`. A program takes and returns all parts, laid end to end along the dimension named above; each array names one. Nothing has to cross between parts.
Inputs may be any that keep to these rules, and one draw needn't show every extreme that they name: `acquired`: every pixel's magnitude, the square root of the sum of its two parts squared, lies between 0.1 and 10.
All inputs are finite; a program needn't handle non-finite values.
Results may differ from a plain program's by a relative error of at most 0.000058.
Values sent between devices are 32-bit elements; how exact they have to be, the bound alone decides.
A program may use at most 64 MiB of HBM per device.

v0:
```python
import jax
import jax.numpy as jnp
from jax import lax
from jax.sharding import PartitionSpec as P

SHIFTS = 4


row_reach = 5
col_reach = 2


def padded(cells, sides, width):
    for axis, dim in sides:
        count = lax.axis_size(axis)
        ends = count - 1
        head = lax.slice_in_dim(cells, 0, width, axis=dim)
        tail = lax.slice_in_dim(cells, cells.shape[dim] - width, cells.shape[dim], axis=dim)
        cells = jnp.concatenate(
            [
                lax.ppermute(tail, axis, [(i, (i + 1) % count) for i in range(ends)]),
                cells,
                lax.ppermute(head, axis, [((i + 1) % count, i) for i in range(ends)]),
            ],
            axis=dim,
        )
    return cells


def passed_along(value, axis, steps):
    count = lax.axis_size(axis)
    pairs = [(source, (source + steps) % count) for source in range(count)]
    return lax.ppermute(value, axis, pairs)


def band_tables(height, breadth):
    first = lax.broadcasted_iota(jnp.int32, (height, height + 2 * row_reach), 0)
    second = lax.broadcasted_iota(jnp.int32, (height, height + 2 * row_reach), 1)
    row_band = ((second >= first) & (second <= first + 2 * row_reach)).astype(jnp.float32)
    left = lax.broadcasted_iota(jnp.int32, (breadth, breadth), 0)
    right = lax.broadcasted_iota(jnp.int32, (breadth, breadth), 1)
    col_band = (jnp.abs(left - right) <= col_reach).astype(jnp.float32)
    return (row_band, col_band)


def box_sum(values_in, row_band, col_band):
    rows_done = jnp.einsum("ir,...rc->...ic", row_band, values_in, precision=lax.Precision.HIGHEST)
    return jnp.einsum("...ic,cd->...id", rows_done, col_band, precision=lax.Precision.HIGHEST)


def block_coherence(anchor, anchor_power, partner, partner_power, row_band, col_band):
    anchor_re = anchor[0][:, None]
    anchor_im = anchor[1][:, None]
    partner_re = partner[0][None]
    partner_im = partner[1][None]
    cross_re = box_sum(anchor_re * partner_re + anchor_im * partner_im, row_band, col_band)
    cross_im = box_sum(anchor_im * partner_re - anchor_re * partner_im, row_band, col_band)
    inverse = lax.rsqrt(anchor_power[:, None] * partner_power[None])
    return jnp.stack([cross_re * inverse, cross_im * inverse])


def on_device(acquired):
    height = acquired.shape[2]
    breadth = acquired.shape[3]
    row_band, col_band = band_tables(height, breadth)
    anchor = padded(acquired, (("tile", 2),), row_reach)
    anchor_power = box_sum(anchor[0] * anchor[0] + anchor[1] * anchor[1], row_band, col_band)
    blocks = [block_coherence(anchor, anchor_power, anchor, anchor_power, row_band, col_band)]
    travel = anchor
    for offset in range(1, SHIFTS):
        travel = passed_along(travel, "date", -1)
        partner_power = box_sum(travel[0] * travel[0] + travel[1] * travel[1], row_band, col_band)
        blocks.append(
            block_coherence(anchor, anchor_power, travel, partner_power, row_band, col_band)
        )
    return jnp.stack(blocks, axis=1)


def solution(mesh):
    in_specs = (P(None, "date", ("groups", "tile"), None),)
    out_specs = P(None, None, "date", None, ("groups", "tile"), None)
    return jax.shard_map(
        on_device, mesh=mesh, in_specs=in_specs, out_specs=out_specs, check_vma=False
    )
```

profile of v0, /device:TPU:70, one launch (start us, length us, event | category | flops | bytes accessed | tf_op | source)
XLA Modules:
  0.0 81.9 jit_solution(10816194121320789480)
XLA Ops:
  0.0 0.9 %fusion.129 = (f32[2,8,5,128]{3,2,1,0:T(8,128)S(1)}, f32[2,8,5,128]{3,2,1,0:T(8,128)S(1)}) fusion(f32[2,8,16,128]{3,2,1,0:T(8,128)} %param.1), kind=kLoop, calls=%fused_computation.159 | loop fusion | bytes 163840 | tf_op jit(solution)/shard_map/slice | solution.py:18
  0.9 4.8 %collective-permute-start = (f32[2,8,5,128]{3,2,1,0:T(8,128)S(1)}, f32[2,8,5,128]{3,2,1,0:T(8,128)S(1)}, u32[]{:S(2)}, u32[]{:S(2)}) collective-permute-start(f32[2,8,5,128]{3,2,1,0:T(8,128)S(1)} %get-tuple-element.13), channel_id=1, source_target_pairs={{0,1},{1,2},{2,3},{3,4},{4,5},{5,6},{6,7},{8,9},{9,10},{10,11},{11... | collective-permute-start | bytes 122888 | tf_op jit(solution)/shard_map/ppermute | solution.py:21
  5.7 2.0 %collective-permute-start.1 = (f32[2,8,5,128]{3,2,1,0:T(8,128)S(1)}, f32[2,8,5,128]{3,2,1,0:T(8,128)S(1)}, u32[]{:S(2)}, u32[]{:S(2)}) collective-permute-start(f32[2,8,5,128]{3,2,1,0:T(8,128)S(1)} %get-tuple-element.14), channel_id=1, source_target_pairs={{1,0},{2,1},{3,2},{4,3},{5,4},{6,5},{7,6},{9,8},{10,9},{11,10},{12... | collective-permute-start | bytes 122888 | tf_op jit(solution)/shard_map/ppermute | solution.py:23
  7.6 0.0 collective-permute-done
  7.6 5.4 %collective-permute-done.1 = f32[2,8,5,128]{3,2,1,0:T(8,128)S(1)} collective-permute-done((f32[2,8,5,128]{3,2,1,0:T(8,128)S(1)}, f32[2,8,5,128]{3,2,1,0:T(8,128)S(1)}, u32[]{:S(2)}, u32[]{:S(2)}) %collective-permute-start.1) | collective-permute-done | bytes 40992 | tf_op jit(solution)/shard_map/ppermute | solution.py:23
  13.1 0.9 %pad_maximum_fusion.1 = f32[2,8,26,128]{3,2,1,0:T(8,128)S(1)} fusion(f32[2,8,5,128]{3,2,1,0:T(8,128)S(1)} %collective-permute-done.1, f32[2,8,16,128]{3,2,1,0:T(8,128)} %param.1, f32[2,8,5,128]{3,2,1,0:T(8,128)S(1)} %collective-permute-done), kind=kLoop, calls=%fused_computation.93 | loop fusion | flops 106496 | bytes 425984 | tf_op jit(solution)/shard_map/concatenate | solution.py:19
  14.0 40.2 %collective-permute-start.2 = (f32[2,8,26,128]{3,2,1,0:T(8,128)S(1)}, f32[2,8,26,128]{3,2,1,0:T(8,128)S(1)}, u32[]{:S(2)}, u32[]{:S(2)}) collective-permute-start(f32[2,8,26,128]{3,2,1,0:T(8,128)S(1)} %pad_maximum_fusion.1), channel_id=1, source_target_pairs={{0,248},{8,0},{16,8},{24,16},{32,24},{40,32},{48,40},{56,48},{64,5... | collective-permute-start | bytes 638984 | tf_op jit(solution)/shard_map/ppermute | solution.py:33
  54.3 0.2 convolution_bitcast_fusion.11
  54.5 0.7 convolution_bitcast_fusion.6
  55.2 0.7 convolution_bitcast_fusion.7
  55.8 0.2 fusion.90
  56.0 0.4 fusion.6
  56.4 0.4 fusion.7
  56.8 1.3 %collective-permute-done.2 = f32[2,8,26,128]{3,2,1,0:T(8,128)S(1)} collective-permute-done((f32[2,8,26,128]{3,2,1,0:T(8,128)S(1)}, f32[2,8,26,128]{3,2,1,0:T(8,128)S(1)}, u32[]{:S(2)}, u32[]{:S(2)}) %collective-permute-start.2) | collective-permute-done | bytes 213024 | tf_op jit(solution)/shard_map/ppermute | solution.py:33
  58.2 0.7 convolution_bitcast_fusion.4
  58.9 0.7 convolution_bitcast_fusion.5
  59.5 0.2 convolution_bitcast_fusion.10
  59.8 0.2 fusion.88
  60.0 0.4 fusion.4
  60.4 3.2 %collective-permute-start.3 = (f32[2,8,26,128]{3,2,1,0:T(8,128)S(1)}, f32[2,8,26,128]{3,2,1,0:T(8,128)S(1)}, u32[]{:S(2)}, u32[]{:S(2)}) collective-permute-start(f32[2,8,26,128]{3,2,1,0:T(8,128)S(1)} %collective-permute-done.2), channel_id=1, source_target_pairs={{0,248},{8,0},{16,8},{24,16},{32,24},{40,32},{48,40},{56,48},{64,5... | collective-permute-start | bytes 638984 | tf_op jit(solution)/shard_map/ppermute | solution.py:33
  63.5 0.4 fusion.5
  63.9 0.1 maximum_bitcast_fusion
  64.1 3.3 %collective-permute-done.3 = f32[2,8,26,128]{3,2,1,0:T(8,128)S(1)} collective-permute-done((f32[2,8,26,128]{3,2,1,0:T(8,128)S(1)}, f32[2,8,26,128]{3,2,1,0:T(8,128)S(1)}, u32[]{:S(2)}, u32[]{:S(2)}) %collective-permute-start.3) | collective-permute-done | bytes 213024 | tf_op jit(solution)/shard_map/ppermute | solution.py:33
  67.4 0.7 convolution_bitcast_fusion.2
  68.1 0.7 convolution_bitcast_fusion.3
  68.8 0.2 convolution_bitcast_fusion.9
  69.1 0.2 fusion.86
  69.2 3.2 %collective-permute-start.4 = (f32[2,8,26,128]{3,2,1,0:T(8,128)S(1)}, f32[2,8,26,128]{3,2,1,0:T(8,128)S(1)}, u32[]{:S(2)}, u32[]{:S(2)}) collective-permute-start(f32[2,8,26,128]{3,2,1,0:T(8,128)S(1)} %collective-permute-done.3), channel_id=1, source_target_pairs={{0,248},{8,0},{16,8},{24,16},{32,24},{40,32},{48,40},{56,48},{64,5... | collective-permute-start | bytes 638984 | tf_op jit(solution)/shard_map/ppermute | solution.py:33
  72.4 0.4 fusion.2
  72.8 0.4 fusion.3
  73.2 3.1 %collective-permute-done.4 = f32[2,8,26,128]{3,2,1,0:T(8,128)S(1)} collective-permute-done((f32[2,8,26,128]{3,2,1,0:T(8,128)S(1)}, f32[2,8,26,128]{3,2,1,0:T(8,128)S(1)}, u32[]{:S(2)}, u32[]{:S(2)}) %collective-permute-start.4) | collective-permute-done | bytes 213024 | tf_op jit(solution)/shard_map/ppermute | solution.py:33
  76.3 0.7 convolution_bitcast_fusion
  77.0 0.7 convolution_bitcast_fusion.1
  77.7 0.2 convolution_bitcast_fusion.8
  77.9 0.2 fusion.84
  78.1 0.4 fusion
  78.5 0.4 fusion.1
  78.9 0.1 maximum_bitcast_fusion.2
  79.1 0.5 pad_maximum_fusion
  79.6 2.3 %copy.2 = f32[2,4,8,8,16,128]{5,4,3,2,1,0:T(8,128)} copy(f32[2,4,8,8,16,128]{5,4,3,2,0,1:T(8,128)S(1)} %pad_maximum_fusion) | data formatting | bytes 8388608 | tf_op jit(solution)/shard_map/stack | solution.py:76
  (5 shorter events, 0.1 us)
Async XLA Ops:
  0.9 6.8 %collective-permute-start = (f32[2,8,5,128]{3,2,1,0:T(8,128)S(1)}, f32[2,8,5,128]{3,2,1,0:T(8,128)S(1)}, u32[]{:S(2)}, u32[]{:S(2)}) collective-permute-start(f32[2,8,5,128]{3,2,1,0:T(8,128)S(1)} %get-tuple-element.13), channel_id=1, source_target_pairs={{0,1},{1,2},{2,3},{3,4},{4,5},{5,6},{6,7},{8,9},{9,10},{10,11},{11... | collective-permute-start | bytes 122888 | tf_op jit(solution)/shard_map/ppermute | solution.py:21
  5.7 7.4 %collective-permute-start.1 = (f32[2,8,5,128]{3,2,1,0:T(8,128)S(1)}, f32[2,8,5,128]{3,2,1,0:T(8,128)S(1)}, u32[]{:S(2)}, u32[]{:S(2)}) collective-permute-start(f32[2,8,5,128]{3,2,1,0:T(8,128)S(1)} %get-tuple-element.14), channel_id=1, source_target_pairs={{1,0},{2,1},{3,2},{4,3},{5,4},{6,5},{7,6},{9,8},{10,9},{11,10},{12... | collective-permute-start | bytes 122888 | tf_op jit(solution)/shard_map/ppermute | solution.py:23
  14.0 44.1 %collective-permute-start.2 = (f32[2,8,26,128]{3,2,1,0:T(8,128)S(1)}, f32[2,8,26,128]{3,2,1,0:T(8,128)S(1)}, u32[]{:S(2)}, u32[]{:S(2)}) collective-permute-start(f32[2,8,26,128]{3,2,1,0:T(8,128)S(1)} %pad_maximum_fusion.1), channel_id=1, source_target_pairs={{0,248},{8,0},{16,8},{24,16},{32,24},{40,32},{48,40},{56,48},{64,5... | collective-permute-start | bytes 638984 | tf_op jit(solution)/shard_map/ppermute | solution.py:33
  60.4 7.1 %collective-permute-start.3 = (f32[2,8,26,128]{3,2,1,0:T(8,128)S(1)}, f32[2,8,26,128]{3,2,1,0:T(8,128)S(1)}, u32[]{:S(2)}, u32[]{:S(2)}) collective-permute-start(f32[2,8,26,128]{3,2,1,0:T(8,128)S(1)} %collective-permute-done.2), channel_id=1, source_target_pairs={{0,248},{8,0},{16,8},{24,16},{32,24},{40,32},{48,40},{56,48},{64,5... | collective-permute-start | bytes 638984 | tf_op jit(solution)/shard_map/ppermute | solution.py:33
  69.2 7.1 %collective-permute-start.4 = (f32[2,8,26,128]{3,2,1,0:T(8,128)S(1)}, f32[2,8,26,128]{3,2,1,0:T(8,128)S(1)}, u32[]{:S(2)}, u32[]{:S(2)}) collective-permute-start(f32[2,8,26,128]{3,2,1,0:T(8,128)S(1)} %collective-permute-done.3), channel_id=1, source_target_pairs={{0,248},{8,0},{16,8},{24,16},{32,24},{40,32},{48,40},{56,48},{64,5... | collective-permute-start | bytes 638984 | tf_op jit(solution)/shard_map/ppermute | solution.py:33
where the time goes:
time: 82.1 us; the launch traced here: 81.9 us
  starting transfers between devices  53.3 us (65%)
  waiting for transfers between devices  13.2 us (16%)
  matrix products  10.2 us (12%)
  local copies, waits for them, and re-layouts  3.27 us (4%)
  other arithmetic  1.7 us (2%)
    ppermute x3, starting transfers between devices, passed_along(): return lax.ppermute(value, axis, pairs)  46.5 us
    ppermute x3, waiting for transfers between devices, passed_along(): return lax.ppermute(value, axis, pairs)  7.77 us
    dot_general x12, matrix products, box_sum(): jnp.einsum('ir,...rc->...ic', row_band, values_in, precision=lax.Precisio...  6.33 us
    ppermute x1, waiting for transfers between devices, padded(): lax.ppermute(head, axis, [((i + 1) % count, i) for i in range(ends)])  5.42 us
    ppermute x1, starting transfers between devices, padded(): lax.ppermute(tail, axis, [(i, (i + 1) % count) for i in range(ends)])  4.78 us
    dot_general x12, matrix products, box_sum(): jnp.einsum('...ic,cd->...id', rows_done, col_band, precision=lax.Precisio...  3.84 us
    another operation x1, local copies, waits for them, and re-layouts, on_device(): return jnp.stack(blocks, axis=1)  2.32 us
    ppermute x1, starting transfers between devices, padded(): lax.ppermute(head, axis, [((i + 1) % count, i) for i in range(ends)])  1.95 us
  transfers between devices with their start and end apart: 5, of which 4 were waited for; matrix products, arithmetic and copies ran while one was open for 5% of the time, Pallas kernels for 0%

commit v1 on v0

v1 whole, which is shorter than its diff:
```python
import functools

import jax
import jax.numpy as jnp
from jax import lax
from jax.experimental import pallas as pl
from jax.experimental.pallas import tpu as pltpu
from jax.sharding import PartitionSpec as P

SHIFTS = 4
row_reach = 5
col_reach = 2
EDGE = 8
MESH = pl.DeviceIdType.MESH


def when(*conditions):
    return pl.when(functools.reduce(jnp.logical_and, conditions))


def exchange_kernel(
    dates, tiles, mine, core, above, below, relay,
    send, got_core, got_above, got_below, relay_send, relay_got, ready,
):
    me = lax.axis_index("date")
    tile = lax.axis_index("tile")
    height = mine.shape[2]
    middle = dates * 9 // 16
    origin = me - middle
    relays = (origin >= 0) & (origin < SHIFTS - 1)
    first = me < SHIFTS - 1

    def there(side):
        return (tile + side >= 0) & (tile + side < tiles)

    routes = [(step, side) for step in range(SHIFTS) for side in (1, -1, 0) if (step, side) != (0, 0)]

    def piece(step, side, source):
        if side == 0:
            return source, core.at[step - 1], got_core.at[step - 1]
        if side == 1:
            return source.at[:, :, pl.ds(height - EDGE, EDGE), :], above.at[step], got_above.at[step]
        return source.at[:, :, pl.ds(0, EDGE), :], below.at[step], got_below.at[step]

    def copy(step, side, source, date, sems):
        src, dst, got = piece(step, side, source)
        return pltpu.make_async_remote_copy(
            src_ref=src, dst_ref=dst, send_sem=sems.at[step, side + 1], recv_sem=got,
            device_id={"date": date, "tile": tile + side}, device_id_type=MESH,
        )

    barrier = pltpu.get_barrier_semaphore()
    count = jnp.int32(0)
    for step, side in routes:
        @when(there(side))
        def _():
            straight = me + step < dates

            @pl.when(straight)
            def _():
                pl.semaphore_signal(
                    barrier, inc=1, device_id={"date": me + step, "tile": tile + side}, device_id_type=MESH)

        count += (there(-side) & (me - step >= 0)).astype(jnp.int32)
        count += (there(side) & (me + step >= dates)).astype(jnp.int32)
    for step, side in routes:
        @when(relays, step > origin, there(side))
        def _():
            pl.semaphore_signal(
                barrier, inc=1, device_id={"date": dates + origin - step, "tile": tile + side}, device_id_type=MESH)

    @pl.when(first)
    def _():
        pl.semaphore_signal(barrier, inc=1, device_id={"date": me + middle, "tile": tile}, device_id_type=MESH)

    count += relays.astype(jnp.int32)
    pl.semaphore_wait(barrier, count)

    for step, side in routes:
        @when(there(side), me - step >= 0)
        def _():
            copy(step, side, mine, me - step, send).start()

    @pl.when(relays)
    def _():
        pl.semaphore_signal(ready, inc=1, device_id={"date": origin, "tile": tile}, device_id_type=MESH)

    for step, side in routes:
        @when(there(side), me + step >= dates)
        def _():
            pl.semaphore_signal(
                ready, inc=1, device_id={"date": me + step - dates + middle, "tile": tile + side}, device_id_type=MESH)

    @pl.when(tile == 0)
    def _():
        above[...] = jnp.zeros_like(above)

    @pl.when(tile == tiles - 1)
    def _():
        below[...] = jnp.zeros_like(below)

    def to_relay():
        return pltpu.make_async_remote_copy(
            src_ref=mine, dst_ref=relay, send_sem=relay_send.at[0, 1], recv_sem=relay_got,
            device_id={"date": me + middle, "tile": tile}, device_id_type=MESH,
        )

    @pl.when(first)
    def _():
        pl.semaphore_wait(ready, 1)
        to_relay().start()

    @pl.when(relays)
    def _():
        count = jnp.int32(0)
        for step, side in routes:
            count += ((step > origin) & there(side)).astype(jnp.int32)
        pl.semaphore_wait(ready, count)
        to_relay().wait_recv()
        for step, side in routes:
            if step:
                @when(step > origin, there(side))
                def _():
                    copy(step, side, relay, dates + origin - step, relay_send).start()

    for step, side in reversed(routes):
        @pl.when(there(-side))
        def _():
            copy(step, side, mine, me, send).wait_recv()

    for step, side in routes:
        @when(there(side), me - step >= 0)
        def _():
            copy(step, side, mine, me - step, send).wait_send()

    @pl.when(first)
    def _():
        to_relay().wait_send()

    for step, side in routes:
        if step:
            @when(relays, step > origin, there(side))
            def _():
                copy(step, side, relay, dates + origin - step, relay_send).wait_send()


def exchange(acquired, dates, tiles):
    parts, block, height, breadth = acquired.shape
    shape = (parts, block, height, breadth)
    edge = (SHIFTS, parts, block, EDGE, breadth)
    return pl.pallas_call(
        functools.partial(exchange_kernel, dates, tiles),
        out_shape=(
            jax.ShapeDtypeStruct((SHIFTS - 1,) + shape, jnp.float32),
            jax.ShapeDtypeStruct(edge, jnp.float32),
            jax.ShapeDtypeStruct(edge, jnp.float32),
        ),
        in_specs=[pl.BlockSpec(memory_space=pl.ANY)],
        out_specs=(pl.BlockSpec(memory_space=pltpu.VMEM),) * 3,
        scratch_shapes=[
            pltpu.VMEM(shape, jnp.float32),
            pltpu.SemaphoreType.DMA((SHIFTS, 3)),
            pltpu.SemaphoreType.DMA((SHIFTS - 1,)),
            pltpu.SemaphoreType.DMA((SHIFTS,)),
            pltpu.SemaphoreType.DMA((SHIFTS,)),
            pltpu.SemaphoreType.DMA((SHIFTS, 3)),
            pltpu.SemaphoreType.DMA,
            pltpu.SemaphoreType.REGULAR,
        ],
        compiler_params=pltpu.CompilerParams(
            collective_id=0, has_side_effects=True, vmem_limit_bytes=8 << 20),
        name="exchange",
    )(acquired)


def window_sums(rows, height):
    width = 2 * row_reach + 1
    sums = [None] * height
    start = 0
    while start < height:
        size = min(width, height - start)
        last = start + width - 1
        tail = rows[last]
        tails = {last: tail}
        for row in range(last - 1, start - 1, -1):
            tail = tail + rows[row]
            tails[row] = tail
        sums[start] = tails[start]
        head = None
        for row in range(start + 1, start + size):
            new = rows[row + width - 1]
            head = new if head is None else head + new
            sums[row] = tails[row] + head
        start += size
    return sums


def coherence_kernel(
    mine, core, above, below, band, out, parts, sums, power, scale, staged, done,
):
    block, height = out.shape[2], out.shape[4]
    breadth = out.shape[5]
    rows = height + 2 * row_reach

    def split_box(values):
        high = values.astype(jnp.bfloat16)
        low = (values - high.astype(jnp.float32)).astype(jnp.bfloat16)
        return jnp.dot(jnp.concatenate([high, low], axis=1), band[...], preferred_element_type=jnp.float32)

    def by_date(ref, part):
        tiles = []
        for date in range(block):
            for at in range(0, height, 8):
                tiles.append(ref[part, pl.ds(at * block + date, 8, stride=block), :])
        return jnp.concatenate(tiles, axis=0)

    for step in range(SHIFTS):
        for part in range(2):
            for row in range(rows):
                if row < row_reach:
                    value = above[step, part, pl.ds(EDGE - row_reach + row, block, stride=EDGE), :]
                elif row < row_reach + height:
                    at = pl.ds(row - row_reach, block, stride=height)
                    value = mine[part, at, :] if step == 0 else core[step - 1, part, at, :]
                else:
                    value = below[step, part, pl.ds(row - row_reach - height, block, stride=EDGE), :]
                parts[step, part, row] = value

    for step in range(SHIFTS):
        squares = [parts[step, 0, row] * parts[step, 0, row] + parts[step, 1, row] * parts[step, 1, row] for row in range(rows)]
        for row, value in enumerate(window_sums(squares, height)):
            power[0, row * block:(row + 1) * block, :] = value
        boxed = split_box(by_date(power, 0))
        scale[step] = lax.rsqrt(boxed).reshape(block, height, breadth)

    def anchor(part, row, date):
        return jnp.broadcast_to(parts[0, part, row, pl.ds(date, 1), :], (block, parts.shape[-1]))

    def cross(step):
        for date in range(block):
            real, imag = [], []
            for row in range(rows):
                first_re, first_im = anchor(0, row, date), anchor(1, row, date)
                second_re, second_im = parts[step, 0, row], parts[step, 1, row]
                real.append(first_re * second_re + first_im * second_im)
                imag.append(first_im * second_re - first_re * second_im)
            for part, values in ((0, real), (1, imag)):
                for row, value in enumerate(window_sums(values, height)):
                    sums[date, part, row * block:(row + 1) * block, :] = value
        for date in range(block):
            weight = scale[0, date][None] * scale[step]
            for part in range(2):
                boxed = split_box(by_date(sums.at[date], part))
                staged[step, part, date] = boxed.reshape(block, height, breadth) * weight

    def copy_out(step):
        return pltpu.make_async_copy(staged.at[step], out.at[:, step], done.at[step])

    @pl.loop(0, SHIFTS)
    def _(step):
        cross(step)
        copy_out(step).start()

    @pl.loop(0, SHIFTS)
    def _(step):
        copy_out(step).wait()


def coherence(mine, core, above, below):
    parts, block, height, breadth = mine.shape
    left = lax.broadcasted_iota(jnp.int32, (2 * breadth, breadth), 0) % breadth
    right = lax.broadcasted_iota(jnp.int32, (2 * breadth, breadth), 1)
    band = (jnp.abs(left - right) <= col_reach).astype(jnp.bfloat16)
    rows = height + 2 * row_reach
    return pl.pallas_call(
        coherence_kernel,
        out_shape=jax.ShapeDtypeStruct((2, SHIFTS, block, block, height, breadth), jnp.float32),
        in_specs=[pl.BlockSpec(memory_space=pltpu.VMEM)] * 5,
        out_specs=pl.BlockSpec(memory_space=pl.ANY),
        scratch_shapes=[
            pltpu.VMEM((SHIFTS, 2, rows, block, breadth), jnp.float32),
            pltpu.VMEM((block, 2, height * block, breadth), jnp.float32),
            pltpu.VMEM((1, height * block, breadth), jnp.float32),
            pltpu.VMEM((SHIFTS, block, height, breadth), jnp.float32),
            pltpu.VMEM((SHIFTS, 2, block, block, height, breadth), jnp.float32),
            pltpu.SemaphoreType.DMA((SHIFTS,)),
        ],
        compiler_params=pltpu.CompilerParams(vmem_limit_bytes=24 << 20),
        name="coherence",
    )(
        mine.reshape(parts, block * height, breadth),
        core.reshape(SHIFTS - 1, parts, block * height, breadth),
        above.reshape(SHIFTS, parts, block * EDGE, breadth),
        below.reshape(SHIFTS, parts, block * EDGE, breadth),
        band,
    )


def solution(mesh):
    def on_device(acquired):
        core, above, below = exchange(acquired, mesh.shape["date"], mesh.shape["tile"])
        return coherence(acquired, core, above, below)

    in_specs = (P(None, "date", ("groups", "tile"), None),)
    out_specs = P(None, None, "date", None, ("groups", "tile"), None)
    return jax.shard_map(
        on_device, mesh=mesh, in_specs=in_specs, out_specs=out_specs, check_vma=False
    )
```

time: 82.1 us -> 62.3 us (0.76)
  the two profiles are of different devices: /device:TPU:70 before, /device:TPU:66 now
where the time goes in v1:
time: 62.3 us; the launch traced here: 62.2 us
  Pallas kernels  60.2 us (97%)
  local copies, waits for them, and re-layouts  1.8 us (3%)
    pallas_call x1, Pallas kernels, exchange(): pl.pallas_call(functools.partial(exchange_kernel, dates, tiles), out_shap...  55.4 us
    pallas_call x1, Pallas kernels, coherence(): pl.pallas_call(coherence_kernel, out_shape=jax.ShapeDtypeStruct((2, SHIFT...  4.77 us
    unnamed x4, local copies, waits for them, and re-layouts  1.8 us

profile of v1, /device:TPU:66, one launch (start us, length us, event | category | flops | bytes accessed | tf_op | source)
XLA Modules:
  0.0 62.2 jit_solution(16663587183720226919)
XLA Ops:
  0.0 0.2 fusion.band
  0.2 0.0 copy-start
  0.2 0.9 %copy-done = f32[2,8,16,128]{3,2,1,0:T(8,128)S(1)} copy-done((f32[2,8,16,128]{3,2,1,0:T(8,128)S(1)}, f32[2,8,16,128]{3,2,1,0:T(8,128)}, u32[]{:S(2)}) %copy-start) | copy-done | bytes 131096
  1.1 55.4 %exchange.1 = (f32[3,2,8,16,128]{4,3,2,1,0:T(8,128)S(1)}, f32[4,2,8,8,128]{4,3,2,1,0:T(8,128)S(1)}, f32[4,2,8,8,128]{4,3,2,1,0:T(8,128)S(1)}) custom-call(f32[2,8,16,128]{3,2,1,0:T(8,128)S(1)} %copy-done), custom_call_target="tpu_custom_call" | custom-call | tf_op jit(solution)/shard_map/exchange/pallas_call | solution.py:151
  56.5 0.0 copy-start.1
  56.5 0.9 %copy-done.1 = f32[2,8,16,128]{3,2,1,0:T(8,128)S(1)} copy-done((f32[2,8,16,128]{3,2,1,0:T(8,128)S(1)}, f32[2,8,16,128]{3,2,1,0:T(8,128)}, u32[]{:S(2)}) %copy-start.1) | copy-done | bytes 131096
  57.4 4.8 %coherence.1 = f32[2,4,8,8,16,128]{5,4,3,2,1,0:T(8,128)} custom-call(f32[2,128,128]{2,1,0:T(8,128)S(1)} %bitcast.4, f32[3,2,128,128]{3,2,1,0:T(8,128)S(1)} %bitcast.5, f32[4,2,64,128]{3,2,1,0:T(8,128)S(1)} %bitcast.6, f32[4,2,64,128]{3,2,1,0:T(8,128)S(1)} %bitcast.7, bf16[256,128]{1,0:T(8,128)(2,1)S(1)} %fusion.band), custom_call_target="tpu_custom_call" | custom-call | tf_op jit(solution)/shard_map/coherence/pallas_call | solution.py:275
  (2 shorter events, 0.0 us)
Async XLA Ops:
  0.2 0.9 %copy-start = (f32[2,8,16,128]{3,2,1,0:T(8,128)S(1)}, f32[2,8,16,128]{3,2,1,0:T(8,128)}, u32[]{:S(2)}) copy-start(f32[2,8,16,128]{3,2,1,0:T(8,128)} %mine.1) | copy-start | bytes 393220
  56.5 0.9 %copy-start.1 = (f32[2,8,16,128]{3,2,1,0:T(8,128)S(1)}, f32[2,8,16,128]{3,2,1,0:T(8,128)}, u32[]{:S(2)}) copy-start(f32[2,8,16,128]{3,2,1,0:T(8,128)} %mine.1) | copy-start | bytes 393220

commit v2 on v1

--- a/solution.py
+++ b/solution.py
@@ -19,21 +19,31 @@
 
 
 def exchange_kernel(
-    dates, tiles, mine, core, above, below, relay,
-    send, got_core, got_above, got_below, relay_send, relay_got, ready,
+    dates, tiles, mine, own, core, above, below, relay,
+    send, got_own, got_core, got_above, got_below, relay_send, relay_got, late_send, ready, late_ready,
 ):
     me = lax.axis_index("date")
     tile = lax.axis_index("tile")
     height = mine.shape[2]
-    middle = dates * 9 // 16
-    origin = me - middle
-    relays = (origin >= 0) & (origin < SHIFTS - 1)
-    first = me < SHIFTS - 1
+    near, far = dates * 5 // 16, dates * 3 // 4
+    near_block, far_block = me - near, me - far
+    starts = me < SHIFTS
+    is_near = (near_block >= 0) & (near_block < SHIFTS)
+    is_far = (far_block >= 0) & (far_block < SHIFTS - 1)
 
     def there(side):
         return (tile + side >= 0) & (tile + side < tiles)
 
+    def is_first(date, at):
+        return (date == 0) & (at == 0)
+
+    first = is_first(me, tile)
     routes = [(step, side) for step in range(SHIFTS) for side in (1, -1, 0) if (step, side) != (0, 0)]
+    late = [(step, side) for step, side in routes if side < 1]
+
+    def signal(semaphore, date, side=0):
+        pl.semaphore_signal(
+            semaphore, inc=1, device_id={"date": date, "tile": tile + side}, device_id_type=MESH)
 
     def piece(step, side, source):
         if side == 0:
@@ -49,47 +59,72 @@
             device_id={"date": date, "tile": tile + side}, device_id_type=MESH,
         )
 
+    def straight(step, side):
+        return there(side) & (me >= step) & ~is_first(me - step, tile + side)
+
+    def around(step, side):
+        return is_far & (step > far_block) & there(side)
+
+    def to_first(step, side):
+        return is_near & (near_block == step) & (tile + side == 0)
+
     barrier = pltpu.get_barrier_semaphore()
     count = jnp.int32(0)
     for step, side in routes:
-        @when(there(side))
-        def _():
-            straight = me + step < dates
-
-            @pl.when(straight)
-            def _():
-                pl.semaphore_signal(
-                    barrier, inc=1, device_id={"date": me + step, "tile": tile + side}, device_id_type=MESH)
-
-        count += (there(-side) & (me - step >= 0)).astype(jnp.int32)
+        @when(there(side), me + step < dates, ~first)
+        def _():
+            signal(barrier, me + step, side)
+
+        count += straight(step, side).astype(jnp.int32)
         count += (there(side) & (me + step >= dates)).astype(jnp.int32)
+
+        @pl.when(around(step, side))
+        def _():
+            signal(barrier, dates + far_block - step, side)
+
+    for step, side in late:
+        count += (first & there(-side)).astype(jnp.int32)
+
+        @pl.when(to_first(step, side))
+        def _():
+            signal(barrier, 0, side)
+
+    @pl.when(starts)
+    def _():
+        signal(barrier, me + near)
+
+    @when(is_near, near_block < SHIFTS - 1)
+    def _():
+        signal(barrier, near_block + far)
+
+    count += is_near.astype(jnp.int32) + is_far.astype(jnp.int32)
+    pl.semaphore_wait(barrier, count)
+
     for step, side in routes:
-        @when(relays, step > origin, there(side))
-        def _():
-            pl.semaphore_signal(
-                barrier, inc=1, device_id={"date": dates + origin - step, "tile": tile + side}, device_id_type=MESH)
-
-    @pl.when(first)
-    def _():
-        pl.semaphore_signal(barrier, inc=1, device_id={"date": me + middle, "tile": tile}, device_id_type=MESH)
-
-    count += relays.astype(jnp.int32)
-    pl.semaphore_wait(barrier, count)
-
-    for step, side in routes:
-        @when(there(side), me - step >= 0)
+        @pl.when(straight(step, side))
         def _():
             copy(step, side, mine, me - step, send).start()
 
-    @pl.when(relays)
-    def _():
-        pl.semaphore_signal(ready, inc=1, device_id={"date": origin, "tile": tile}, device_id_type=MESH)
+    keep = pltpu.make_async_copy(mine, own, got_own)
+    keep.start()
+
+    @pl.when(is_near)
+    def _():
+        signal(ready, near_block)
+
+    @pl.when(is_far)
+    def _():
+        signal(ready, far_block + near)
 
     for step, side in routes:
         @when(there(side), me + step >= dates)
         def _():
-            pl.semaphore_signal(
-                ready, inc=1, device_id={"date": me + step - dates + middle, "tile": tile + side}, device_id_type=MESH)
+            signal(ready, me + step - dates + far, side)
+
+    for step, side in late:
+        @when(first, there(-side))
+        def _():
+            signal(late_ready, step + near, -side)
 
     @pl.when(tile == 0)
     def _():
@@ -99,78 +134,102 @@
     def _():
         below[...] = jnp.zeros_like(below)
 
-    def to_relay():
+    def to_relay(source, date):
         return pltpu.make_async_remote_copy(
-            src_ref=mine, dst_ref=relay, send_sem=relay_send.at[0, 1], recv_sem=relay_got,
-            device_id={"date": me + middle, "tile": tile}, device_id_type=MESH,
+            src_ref=source, dst_ref=relay, send_sem=relay_send.at[0, 1], recv_sem=relay_got,
+            device_id={"date": date, "tile": tile}, device_id_type=MESH,
         )
 
-    @pl.when(first)
+    @pl.when(starts)
     def _():
         pl.semaphore_wait(ready, 1)
-        to_relay().start()
-
-    @pl.when(relays)
+        to_relay(mine, me + near).start()
+
+    @pl.when(is_near | is_far)
+    def _():
+        to_relay(mine, me).wait_recv()
+
+    @when(is_near, near_block < SHIFTS - 1)
+    def _():
+        pl.semaphore_wait(ready, 1)
+        to_relay(relay, near_block + far).start()
+
+    for step, side in late:
+        @pl.when(to_first(step, side))
+        def _():
+            pl.semaphore_wait(late_ready, 1)
+            copy(step, side, relay, 0, late_send).start()
+
+    @pl.when(is_far)
     def _():
         count = jnp.int32(0)
         for step, side in routes:
-            count += ((step > origin) & there(side)).astype(jnp.int32)
+            count += around(step, side).astype(jnp.int32)
         pl.semaphore_wait(ready, count)
-        to_relay().wait_recv()
         for step, side in routes:
             if step:
-                @when(step > origin, there(side))
+                @pl.when(around(step, side))
                 def _():
-                    copy(step, side, relay, dates + origin - step, relay_send).start()
+                    copy(step, side, relay, dates + far_block - step, relay_send).start()
 
     for step, side in reversed(routes):
         @pl.when(there(-side))
         def _():
             copy(step, side, mine, me, send).wait_recv()
 
+    keep.wait()
+
     for step, side in routes:
-        @when(there(side), me - step >= 0)
+        @pl.when(straight(step, side))
         def _():
             copy(step, side, mine, me - step, send).wait_send()
 
-    @pl.when(first)
-    def _():
-        to_relay().wait_send()
-
-    for step, side in routes:
         if step:
-            @when(relays, step > origin, there(side))
+            @pl.when(around(step, side))
             def _():
-                copy(step, side, relay, dates + origin - step, relay_send).wait_send()
+                copy(step, side, relay, dates + far_block - step, relay_send).wait_send()
+
+    for step, side in late:
+        @pl.when(to_first(step, side))
+        def _():
+            copy(step, side, relay, 0, late_send).wait_send()
+
+    @pl.when(starts | (is_near & (near_block < SHIFTS - 1)))
+    def _():
+        to_relay(mine, me).wait_send()
 
 
 def exchange(acquired, dates, tiles):
-    parts, block, height, breadth = acquired.shape
-    shape = (parts, block, height, breadth)
+    shape = acquired.shape
+    parts, block, height, breadth = shape
     edge = (SHIFTS, parts, block, EDGE, breadth)
     return pl.pallas_call(
         functools.partial(exchange_kernel, dates, tiles),
         out_shape=(
+            jax.ShapeDtypeStruct(shape, jnp.float32),
             jax.ShapeDtypeStruct((SHIFTS - 1,) + shape, jnp.float32),
             jax.ShapeDtypeStruct(edge, jnp.float32),
             jax.ShapeDtypeStruct(edge, jnp.float32),
         ),
-        in_specs=[pl.BlockSpec(memory_space=pl.ANY)],
-        out_specs=(pl.BlockSpec(memory_space=pltpu.VMEM),) * 3,
+        in_specs=[pl.BlockSpec(memory_space=pltpu.HBM)],
+        out_specs=(pl.BlockSpec(memory_space=pltpu.VMEM),) * 4,
         scratch_shapes=[
             pltpu.VMEM(shape, jnp.float32),
             pltpu.SemaphoreType.DMA((SHIFTS, 3)),
+            pltpu.SemaphoreType.DMA,
             pltpu.SemaphoreType.DMA((SHIFTS - 1,)),
             pltpu.SemaphoreType.DMA((SHIFTS,)),
             pltpu.SemaphoreType.DMA((SHIFTS,)),
             pltpu.SemaphoreType.DMA((SHIFTS, 3)),
             pltpu.SemaphoreType.DMA,
+            pltpu.SemaphoreType.DMA((SHIFTS, 3)),
+            pltpu.SemaphoreType.REGULAR,
             pltpu.SemaphoreType.REGULAR,
         ],
         compiler_params=pltpu.CompilerParams(
             collective_id=0, has_side_effects=True, vmem_limit_bytes=8 << 20),
         name="exchange",
-    )(acquired)
+    )(pltpu.with_memory_space_constraint(acquired, pltpu.HBM))
 
 
 def window_sums(rows, height):
@@ -196,16 +255,20 @@
 
 
 def coherence_kernel(
-    mine, core, above, below, band, out, parts, sums, power, scale, staged, done,
+    mine, core, above, below, out, parts, sums, power, scale, staged, done,
 ):
     block, height = out.shape[2], out.shape[4]
     breadth = out.shape[5]
     rows = height + 2 * row_reach
+    left = lax.broadcasted_iota(jnp.int32, (breadth, breadth), 0)
+    right = lax.broadcasted_iota(jnp.int32, (breadth, breadth), 1)
+    band = (jnp.abs(left - right) <= col_reach).astype(jnp.float32).astype(jnp.bfloat16)
+    band = jnp.concatenate([band, band], axis=0)
 
     def split_box(values):
         high = values.astype(jnp.bfloat16)
         low = (values - high.astype(jnp.float32)).astype(jnp.bfloat16)
-        return jnp.dot(jnp.concatenate([high, low], axis=1), band[...], preferred_element_type=jnp.float32)
+        return jnp.dot(jnp.concatenate([high, low], axis=1), band, preferred_element_type=jnp.float32)
 
     def by_date(ref, part):
         tiles = []
@@ -268,14 +331,11 @@
 
 def coherence(mine, core, above, below):
     parts, block, height, breadth = mine.shape
-    left = lax.broadcasted_iota(jnp.int32, (2 * breadth, breadth), 0) % breadth
-    right = lax.broadcasted_iota(jnp.int32, (2 * breadth, breadth), 1)
-    band = (jnp.abs(left - right) <= col_reach).astype(jnp.bfloat16)
     rows = height + 2 * row_reach
     return pl.pallas_call(
         coherence_kernel,
         out_shape=jax.ShapeDtypeStruct((2, SHIFTS, block, block, height, breadth), jnp.float32),
-        in_specs=[pl.BlockSpec(memory_space=pltpu.VMEM)] * 5,
+        in_specs=[pl.BlockSpec(memory_space=pltpu.VMEM)] * 4,
         out_specs=pl.BlockSpec(memory_space=pl.ANY),
         scratch_shapes=[
             pltpu.VMEM((SHIFTS, 2, rows, block, breadth), jnp.float32),
@@ -292,14 +352,13 @@
         core.reshape(SHIFTS - 1, parts, block * height, breadth),
         above.reshape(SHIFTS, parts, block * EDGE, breadth),
         below.reshape(SHIFTS, parts, block * EDGE, breadth),
-        band,
     )
 
 
 def solution(mesh):
     def on_device(acquired):
-        core, above, below = exchange(acquired, mesh.shape["date"], mesh.shape["tile"])
-        return coherence(acquired, core, above, below)
+        own, core, above, below = exchange(acquired, mesh.shape["date"], mesh.shape["tile"])
+        return coherence(own, core, above, below)
 
     in_specs = (P(None, "date", ("groups", "tile"), None),)
     out_specs = P(None, None, "date", None, ("groups", "tile"), None)

time: 62.3 us -> 55.8 us (0.90)
  the two profiles are of different devices: /device:TPU:66 before, /device:TPU:80 now
where the time goes in v2:
time: 55.8 us; the launch traced here: 55.7 us
  Pallas kernels  55.7 us (100%)
    pallas_call x1, Pallas kernels, exchange(): pl.pallas_call(functools.partial(exchange_kernel, dates, tiles), out_shap...  51.1 us
    pallas_call x1, Pallas kernels, coherence(): pl.pallas_call(coherence_kernel, out_shape=jax.ShapeDtypeStruct((2, SHIFT...  4.62 us

profile of v2, /device:TPU:80, one launch (start us, length us, event | category | flops | bytes accessed | tf_op | source)
XLA Modules:
  0.0 55.7 jit_solution(18108442082245094380)
XLA Ops:
  0.0 51.1 %exchange.1 = (f32[2,8,16,128]{3,2,1,0:T(8,128)S(1)}, f32[3,2,8,16,128]{4,3,2,1,0:T(8,128)S(1)}, f32[4,2,8,8,128]{4,3,2,1,0:T(8,128)S(1)}, f32[4,2,8,8,128]{4,3,2,1,0:T(8,128)S(1)}) custom-call(f32[2,8,16,128]{3,2,1,0:T(8,128)} %mine.1), custom_call_target="tpu_custom_call" | custom-call | tf_op jit(solution)/shard_map/exchange/pallas_call | solution.py:206
  51.1 4.6 %coherence.1 = f32[2,4,8,8,16,128]{5,4,3,2,1,0:T(8,128)} custom-call(f32[2,128,128]{2,1,0:T(8,128)S(1)} %bitcast.7, f32[3,2,128,128]{3,2,1,0:T(8,128)S(1)} %bitcast.4, f32[4,2,64,128]{3,2,1,0:T(8,128)S(1)} %bitcast.5, f32[4,2,64,128]{3,2,1,0:T(8,128)S(1)} %bitcast.6), custom_call_target="tpu_custom_call" | custom-call | tf_op jit(solution)/shard_map/coherence/pallas_call | solution.py:335

commit v3 on v2

--- a/solution.py
+++ b/solution.py
@@ -89,7 +89,14 @@
         def _():
             signal(barrier, 0, side)
 
-    @pl.when(starts)
+    from_first = is_first(near_block, tile)
+    count += first.astype(jnp.int32)
+
+    @pl.when(from_first)
+    def _():
+        signal(barrier, 0)
+
+    @when(starts, ~first)
     def _():
         signal(barrier, me + near)
 
@@ -97,7 +104,7 @@
     def _():
         signal(barrier, near_block + far)
 
-    count += is_near.astype(jnp.int32) + is_far.astype(jnp.int32)
+    count += (is_near & ~from_first).astype(jnp.int32) + is_far.astype(jnp.int32)
     pl.semaphore_wait(barrier, count)
 
     for step, side in routes:
@@ -108,7 +115,7 @@
     keep = pltpu.make_async_copy(mine, own, got_own)
     keep.start()
 
-    @pl.when(is_near)
+    @when(is_near, ~from_first)
     def _():
         signal(ready, near_block)
 
@@ -140,25 +147,28 @@
             device_id={"date": date, "tile": tile}, device_id_type=MESH,
         )
 
+    @when(starts, ~first)
+    def _():
+        pl.semaphore_wait(ready, 1)
+
     @pl.when(starts)
     def _():
-        pl.semaphore_wait(ready, 1)
         to_relay(mine, me + near).start()
 
     @pl.when(is_near | is_far)
     def _():
         to_relay(mine, me).wait_recv()
+
+    for step, side in late:
+        @pl.when(to_first(step, side))
+        def _():
+            pl.semaphore_wait(late_ready, 1)
+            copy(step, side, relay, 0, late_send).start()
 
     @when(is_near, near_block < SHIFTS - 1)
     def _():
         pl.semaphore_wait(ready, 1)
         to_relay(relay, near_block + far).start()
-
-    for step, side in late:
-        @pl.when(to_first(step, side))
-        def _():
-            pl.semaphore_wait(late_ready, 1)
-            copy(step, side, relay, 0, late_send).start()
 
     @pl.when(is_far)
     def _():

time: 55.8 us -> 51.2 us (0.918)
  Pallas kernels: 55.7 us -> 51.1 us
    pallas_call x1, Pallas kernels: 51.1 us -> 46.5 us  [exchange(): pl.pallas_call(functools.partial(exchange_kernel, dates, tiles), out_shap...]
where the time goes in v3:
time: 51.2 us; the launch traced here: 51.1 us
  Pallas kernels  51.1 us (100%)
    pallas_call x1, Pallas kernels, exchange(): pl.pallas_call(functools.partial(exchange_kernel, dates, tiles), out_shap...  46.5 us
    pallas_call x1, Pallas kernels, coherence(): pl.pallas_call(coherence_kernel, out_shape=jax.ShapeDtypeStruct((2, SHIFT...  4.62 us

profile of v3, /device:TPU:80, one launch (start us, length us, event | category | flops | bytes accessed | tf_op | source)
XLA Modules:
  0.0 51.1 jit_solution(3465786232889712318)
XLA Ops:
  0.0 46.5 %exchange.1 = (f32[2,8,16,128]{3,2,1,0:T(8,128)S(1)}, f32[3,2,8,16,128]{4,3,2,1,0:T(8,128)S(1)}, f32[4,2,8,8,128]{4,3,2,1,0:T(8,128)S(1)}, f32[4,2,8,8,128]{4,3,2,1,0:T(8,128)S(1)}) custom-call(f32[2,8,16,128]{3,2,1,0:T(8,128)} %mine.1), custom_call_target="tpu_custom_call" | custom-call | tf_op jit(solution)/shard_map/exchange/pallas_call | solution.py:216
  46.5 4.6 %coherence.1 = f32[2,4,8,8,16,128]{5,4,3,2,1,0:T(8,128)} custom-call(f32[2,128,128]{2,1,0:T(8,128)S(1)} %bitcast.7, f32[3,2,128,128]{3,2,1,0:T(8,128)S(1)} %bitcast.4, f32[4,2,64,128]{3,2,1,0:T(8,128)S(1)} %bitcast.5, f32[4,2,64,128]{3,2,1,0:T(8,128)S(1)} %bitcast.6), custom_call_target="tpu_custom_call" | custom-call | tf_op jit(solution)/shard_map/coherence/pallas_call | solution.py:345

commit v4 on v3

v4 whole, which is shorter than its diff:
```python
import functools

import jax
import jax.numpy as jnp
from jax import lax
from jax.experimental import pallas as pl
from jax.experimental.pallas import tpu as pltpu
from jax.sharding import PartitionSpec as P

SHIFTS = 4
row_reach = 5
col_reach = 2
EDGE = 8
MESH = pl.DeviceIdType.MESH


def when(*conditions):
    return pl.when(functools.reduce(jnp.logical_and, conditions))


def exchange_kernel(
    dates, tiles, mine, above, rows, boxed, partial, partial_power, scale, own, core, below, relay, sums,
    send, got_own, got_core, got_above, got_below, relay_send, relay_got, late_send, ready, late_ready,
):
    me = lax.axis_index("date")
    tile = lax.axis_index("tile")
    block, height, breadth = mine.shape[1:]
    near, far = dates * 5 // 16, dates * 3 // 4
    near_block, far_block = me - near, me - far
    starts = me < SHIFTS
    is_near = (near_block >= 0) & (near_block < SHIFTS)
    is_far = (far_block >= 0) & (far_block < SHIFTS - 1)

    def there(side):
        return (tile + side >= 0) & (tile + side < tiles)

    def is_first(date, at):
        return (lax.axis_index("groups") == 0) & (date == 0) & (at == 0)

    first = is_first(me, tile)
    routes = [(step, side) for step in range(SHIFTS) for side in (1, -1, 0) if (step, side) != (0, 0)]
    late = [(step, side) for step, side in routes if side < 1]

    def signal(semaphore, date, side=0):
        pl.semaphore_signal(
            semaphore, inc=1, device_id={"date": date, "tile": tile + side}, device_id_type=MESH)

    def piece(step, side, source):
        if side == 0:
            return source, core.at[step - 1], got_core.at[step - 1]
        if side == 1:
            return source.at[:, :, pl.ds(height - EDGE, EDGE), :], above.at[step], got_above.at[step]
        return source.at[:, :, pl.ds(0, EDGE), :], below.at[step], got_below.at[step]

    def copy(step, side, source, date, sems):
        src, dst, got = piece(step, side, source)
        return pltpu.make_async_remote_copy(
            src_ref=src, dst_ref=dst, send_sem=sems.at[step, side + 1], recv_sem=got,
            device_id={"date": date, "tile": tile + side}, device_id_type=MESH,
        )

    def straight(step, side):
        return there(side) & (me >= step) & ~is_first(me - step, tile + side)

    def around(step, side):
        return is_far & (step > far_block) & there(side)

    def to_first(step, side):
        return is_near & (near_block == step) & is_first(0, tile + side)

    barrier = pltpu.get_barrier_semaphore()
    count = jnp.int32(0)
    for step, side in routes:
        @when(there(side), me + step < dates, ~first)
        def _():
            signal(barrier, me + step, side)

        count += straight(step, side).astype(jnp.int32)
        count += (there(side) & (me + step >= dates)).astype(jnp.int32)

        @pl.when(around(step, side))
        def _():
            signal(barrier, dates + far_block - step, side)

    for step, side in late:
        count += (first & there(-side)).astype(jnp.int32)

        @pl.when(to_first(step, side))
        def _():
            signal(barrier, 0, side)

    from_first = is_first(near_block, tile)
    count += first.astype(jnp.int32)

    @pl.when(from_first)
    def _():
        signal(barrier, 0)

    @when(starts, ~first)
    def _():
        signal(barrier, me + near)

    @when(is_near, near_block < SHIFTS - 1)
    def _():
        signal(barrier, near_block + far)

    count += (is_near & ~from_first).astype(jnp.int32) + is_far.astype(jnp.int32)
    pl.semaphore_wait(barrier, count)

    for step, side in routes:
        @pl.when(straight(step, side))
        def _():
            copy(step, side, mine, me - step, send).start()

    keep = pltpu.make_async_copy(mine, own, got_own)
    keep.start()

    @when(is_near, ~from_first)
    def _():
        signal(ready, near_block)

    @pl.when(is_far)
    def _():
        signal(ready, far_block + near)

    for step, side in routes:
        @when(there(side), me + step >= dates)
        def _():
            signal(ready, me + step - dates + far, side)

    for step, side in late:
        @when(first, there(-side))
        def _():
            signal(late_ready, step + near, -side)

    @pl.when(tile == 0)
    def _():
        above[...] = jnp.zeros_like(above)

    @pl.when(tile == tiles - 1)
    def _():
        below[...] = jnp.zeros_like(below)

    def to_relay(source, date):
        return pltpu.make_async_remote_copy(
            src_ref=source, dst_ref=relay, send_sem=relay_send.at[0, 1], recv_sem=relay_got,
            device_id={"date": date, "tile": tile}, device_id_type=MESH,
        )

    @pl.when(first)
    def _():
        to_relay(mine, near).start()

    @pl.when(is_far)
    def _():
        to_relay(mine, me).wait_recv()
        count = jnp.int32(0)
        for step, side in routes:
            count += around(step, side).astype(jnp.int32)
        pl.semaphore_wait(ready, count)
        for step, side in routes:
            if step:
                @pl.when(around(step, side))
                def _():
                    copy(step, side, relay, dates + far_block - step, relay_send).start()

    for step, side in reversed(routes):
        if (step, side) != (0, 1):
            @pl.when(there(-side))
            def _():
                copy(step, side, mine, me, send).wait_recv()

    keep.wait()

    band = band_table(breadth)
    total = height + 2 * row_reach
    above_rows = above.reshape(SHIFTS, 2, block * EDGE, breadth)
    below_rows = below.reshape(SHIFTS, 2, block * EDGE, breadth)
    own_rows = own.reshape(2, block * height, breadth)
    core_rows = core.reshape(SHIFTS - 1, 2, block * height, breadth)

    for step in range(SHIFTS):
        for part in range(2):
            for row in range(row_reach):
                rows[step, part, row_reach + height + row] = below_rows[step, part, pl.ds(row, block, stride=EDGE), :]
                if step:
                    at = pl.ds(EDGE - row_reach + row, block, stride=EDGE)
                    rows[step, part, row] = above_rows[step, part, at, :]

    for row in range(height):
        for part in range(2):
            at = pl.ds(row, block, stride=height)
            rows[0, part, row_reach + row] = own_rows[part, at, :]
            for step in range(1, SHIFTS):
                rows[step, part, row_reach + row] = core_rows[step - 1, part, at, :]

    def store(values, ref):
        for row, value in enumerate(values):
            ref[row * block:(row + 1) * block, :] = value

    for step in range(SHIFTS):
        squares = {row: square(rows, step, row) for row in range(row_reach if step == 0 else 0, total)}
        if step == 0:
            store(inner_sums(squares, EDGE), partial_power)
        else:
            store(window_sums(squares, 0, EDGE), sums.at[0])
            scale[step, 0] = lax.rsqrt(box_columns(by_date(sums.at[0], block), band)).reshape(block, EDGE, breadth)
        store(window_sums(squares, EDGE, height), sums.at[1])
        scale[step, 1] = lax.rsqrt(box_columns(by_date(sums.at[1], block), band)).reshape(block, EDGE, breadth)

    @pl.loop(0, SHIFTS)
    def _(step):
        for date in range(block):
            real, imag = products(rows, rows, step, date, range(row_reach, total))
            for part, values in enumerate((real, imag)):
                store(inner_sums(values, EDGE), partial.at[step, date, part])
                store(window_sums(values, EDGE, height), sums.at[date * 2 + part])
        for date in range(block):
            weight = scale[0, 1, date][None] * scale[step, 1]
            for part in range(2):
                columns = box_columns(by_date(sums.at[date * 2 + part], block), band)
                boxed[part, step, date] = columns.reshape(block, EDGE, breadth) * weight

    @when(starts, ~first)
    def _():
        pl.semaphore_wait(ready, 1)
        to_relay(mine, me + near).start()

    for step, side in late:
        @pl.when(to_first(step, side))
        def _():
            to_relay(mine, me).wait_recv()
            pl.semaphore_wait(late_ready, 1)
            copy(step, side, relay, 0, late_send).start()

    serves_first = functools.reduce(jnp.logical_or, [to_first(step, side) for step, side in late])

    @when(is_near, ~serves_first)
    def _():
        to_relay(mine, me).wait_recv()

    @when(is_near, near_block < SHIFTS - 1)
    def _():
        pl.semaphore_wait(ready, 1)
        to_relay(relay, near_block + far).start()

    @pl.when(there(-1))
    def _():
        copy(0, 1, mine, me, send).wait_recv()

    for step, side in routes:
        @pl.when(straight(step, side))
        def _():
            copy(step, side, mine, me - step, send).wait_send()

        if step:
            @pl.when(around(step, side))
            def _():
                copy(step, side, relay, dates + far_block - step, relay_send).wait_send()

    for step, side in late:
        @pl.when(to_first(step, side))
        def _():
            copy(step, side, relay, 0, late_send).wait_send()

    @pl.when(starts | (is_near & (near_block < SHIFTS - 1)))
    def _():
        to_relay(mine, me).wait_send()


def exchange(acquired, dates, tiles):
    parts, block, height, breadth = acquired.shape
    total = height + 2 * row_reach
    edge = (SHIFTS, parts, block, EDGE, breadth)
    results = (
        edge,
        (SHIFTS, parts, total, block, breadth),
        (2, SHIFTS, block, block, EDGE, breadth),
        (SHIFTS, block, 2, EDGE * block, breadth),
        (EDGE * block, breadth),
        (SHIFTS, 2, block, EDGE, breadth),
    )
    return pl.pallas_call(
        functools.partial(exchange_kernel, dates, tiles),
        out_shape=tuple(jax.ShapeDtypeStruct(shape, jnp.float32) for shape in results),
        in_specs=[pl.BlockSpec(memory_space=pltpu.HBM)],
        out_specs=(pl.BlockSpec(memory_space=pltpu.VMEM),) * len(results),
        scratch_shapes=[
            pltpu.VMEM(acquired.shape, jnp.float32),
            pltpu.VMEM((SHIFTS - 1,) + acquired.shape, jnp.float32),
            pltpu.VMEM(edge, jnp.float32),
            pltpu.VMEM(acquired.shape, jnp.float32),
            pltpu.VMEM((2 * block, EDGE * block, breadth), jnp.float32),
            pltpu.SemaphoreType.DMA((SHIFTS, 3)),
            pltpu.SemaphoreType.DMA,
            pltpu.SemaphoreType.DMA((SHIFTS - 1,)),
            pltpu.SemaphoreType.DMA((SHIFTS,)),
            pltpu.SemaphoreType.DMA((SHIFTS,)),
            pltpu.SemaphoreType.DMA((SHIFTS, 3)),
            pltpu.SemaphoreType.DMA,
            pltpu.SemaphoreType.DMA((SHIFTS, 3)),
            pltpu.SemaphoreType.REGULAR,
            pltpu.SemaphoreType.REGULAR,
        ],
        compiler_params=pltpu.CompilerParams(
            collective_id=0, has_side_effects=True, vmem_limit_bytes=16 << 20),
        name="exchange",
    )(pltpu.with_memory_space_constraint(acquired, pltpu.HBM))


def band_table(breadth):
    left = lax.broadcasted_iota(jnp.int32, (breadth, breadth), 0)
    right = lax.broadcasted_iota(jnp.int32, (breadth, breadth), 1)
    band = (jnp.abs(left - right) <= col_reach).astype(jnp.float32).astype(jnp.bfloat16)
    return jnp.concatenate([band, band], axis=0)


def box_columns(values, band):
    high = values.astype(jnp.bfloat16)
    low = (values - high.astype(jnp.float32)).astype(jnp.bfloat16)
    return jnp.dot(jnp.concatenate([high, low], axis=1), band, preferred_element_type=jnp.float32)


def by_date(ref, block):
    return jnp.concatenate([ref[pl.ds(date, EDGE, stride=block), :] for date in range(block)], axis=0)


def square(rows, step, row):
    real, imag = rows[step, 0, row], rows[step, 1, row]
    return real * real + imag * imag


def products(first, second, step, date, which):
    real, imag = {}, {}
    for row in which:
        second_re, second_im = second[step, 0, row], second[step, 1, row]
        first_re = jnp.broadcast_to(first[0, 0, row, pl.ds(date, 1), :], second_re.shape)
        first_im = jnp.broadcast_to(first[0, 1, row, pl.ds(date, 1), :], second_re.shape)
        real[row] = first_re * second_re + first_im * second_im
        imag[row] = first_im * second_re - first_re * second_im
    return real, imag


def window_sums(rows, start, stop):
    last = start + 2 * row_reach
    tails = {last: rows[last]}
    for row in range(last - 1, start - 1, -1):
        tails[row] = tails[row + 1] + rows[row]
    sums, head = [tails[start]], None
    for row in range(start + 1, stop):
        new = rows[row + 2 * row_reach]
        head = new if head is None else head + new
        sums.append(tails[row] + head)
    return sums


def inner_sums(rows, count):
    last = 2 * row_reach
    tails = {last: rows[last]}
    for row in range(last - 1, row_reach - 1, -1):
        tails[row] = tails[row + 1] + rows[row]
    sums, head = [tails[row_reach]], None
    for row in range(1, count):
        new = rows[row + last]
        head = new if head is None else head + new
        sums.append(tails[max(row, row_reach)] + head)
    return sums


def coherence_kernel(
    above, rows, boxed, partial, partial_power, scale, out, top, sums, weights, staged, done, done_boxed,
):
    block, breadth = out.shape[2], out.shape[5]
    finished = pltpu.make_async_copy(boxed, out.at[:, :, :, :, pl.ds(EDGE, EDGE), :], done_boxed)
    finished.start()
    band = band_table(breadth)
    which = range(row_reach)
    above = above.reshape(SHIFTS, 2, block * EDGE, breadth)

    for part in range(2):
        for row in which:
            top[0, part, row] = above[0, part, pl.ds(EDGE - row_reach + row, block, stride=EDGE), :]
            for step in range(1, SHIFTS):
                top[step, part, row] = rows[step, part, row]

    def add_top(values, inner, ref):
        tail = None
        for row in reversed(which):
            tail = values[row] if tail is None else tail + values[row]
            at = pl.ds(row * block, block)
            ref[at, :] = inner[at, :] + tail
        at = pl.ds(row_reach * block, (EDGE - row_reach) * block)
        ref[at, :] = inner[at, :]

    add_top({row: square(top, 0, row) for row in which}, partial_power, sums.at[0])
    weights[0] = lax.rsqrt(box_columns(by_date(sums.at[0], block), band)).reshape(block, EDGE, breadth)
    for step in range(1, SHIFTS):
        weights[step] = scale[step, 0]

    def copy_out(step):
        return pltpu.make_async_copy(
            staged.at[step], out.at[:, step, :, :, pl.ds(0, EDGE), :], done.at[step])

    @pl.loop(0, SHIFTS)
    def _(step):
        for date in range(block):
            both = products(top, top, step, date, which)
            for part, values in enumerate(both):
                add_top(values, partial.at[step, date, part], sums.at[date * 2 + part])
        for date in range(block):
            weight = weights[0, date][None] * weights[step]
            for part in range(2):
                columns = box_columns(by_date(sums.at[date * 2 + part], block), band)
                staged[step, part, date] = columns.reshape(block, EDGE, breadth) * weight
        copy_out(step).start()

    @pl.loop(0, SHIFTS)
    def _(step):
        copy_out(step).wait()

    finished.wait()


def coherence(block, height, breadth, *values):
    return pl.pallas_call(
        coherence_kernel,
        out_shape=jax.ShapeDtypeStruct((2, SHIFTS, block, block, height, breadth), jnp.float32),
        in_specs=[pl.BlockSpec(memory_space=pltpu.VMEM)] * len(values),
        out_specs=pl.BlockSpec(memory_space=pl.ANY),
        scratch_shapes=[
            pltpu.VMEM((SHIFTS, 2, row_reach, block, breadth), jnp.float32),
            pltpu.VMEM((2 * block, EDGE * block, breadth), jnp.float32),
            pltpu.VMEM((SHIFTS, block, EDGE, breadth), jnp.float32),
            pltpu.VMEM((SHIFTS, 2, block, block, EDGE, breadth), jnp.float32),
            pltpu.SemaphoreType.DMA((SHIFTS,)),
            pltpu.SemaphoreType.DMA,
        ],
        compiler_params=pltpu.CompilerParams(vmem_limit_bytes=16 << 20),
        name="coherence",
    )(*values)


def solution(mesh):
    def on_device(acquired):
        return coherence(*acquired.shape[1:], *exchange(acquired, mesh.shape["date"], mesh.shape["tile"]))

    in_specs = (P(None, "date", ("groups", "tile"), None),)
    out_specs = P(None, None, "date", None, ("groups", "tile"), None)
    return jax.shard_map(
        on_device, mesh=mesh, in_specs=in_specs, out_specs=out_specs, check_vma=False
    )
```

time: 51.2 us -> 46.8 us (0.914)
  the two profiles are of different devices: /device:TPU:80 before, /device:TPU:66 now
where the time goes in v4:
time: 46.8 us; the launch traced here: 46.7 us
  Pallas kernels  46.7 us (100%)
    pallas_call x1, Pallas kernels, exchange(): pl.pallas_call(functools.partial(exchange_kernel, dates, tiles), out_shap...  44.4 us
    pallas_call x1, Pallas kernels, coherence(): pl.pallas_call(coherence_kernel, out_shape=jax.ShapeDtypeStruct((2, SHIFT...  2.3 us

profile of v4, /device:TPU:66, one launch (start us, length us, event | category | flops | bytes accessed | tf_op | source)
XLA Modules:
  0.0 46.7 jit_solution(11428565334230051875)
XLA Ops:
  0.0 44.4 %exchange.1 = (f32[4,2,8,8,128]{4,3,2,1,0:T(8,128)S(1)}, f32[4,2,26,8,128]{4,3,2,1,0:T(8,128)S(1)}, f32[2,4,8,8,8,128]{5,4,3,2,1,0:T(8,128)S(1)}, f32[4,8,2,64,1...) custom-call(f32[2,8,16,128]{3,2,1,0:T(8,128)} %mine.1), custom_call_target="tpu_custom_call" | custom-call | tf_op jit(solution)/shard_map/exchange/pallas_call | solution.py:283
  44.4 2.3 %coherence.1 = f32[2,4,8,8,16,128]{5,4,3,2,1,0:T(8,128)} custom-call(f32[4,2,8,8,128]{4,3,2,1,0:T(8,128)S(1)} %get-tuple-element.11.above, f32[4,2,26,8,128]{4,3,2,1,0:T(8,128)S(1)} %get-tuple-element.12.rows, f32[2,4,8,8,8,128]{5,4,3,2,1,0:T(8,128)S(1)} %get-tuple-element.13.boxed, f32[4,8,2,64,128]{4,3,2,1,0:T(8,128)S(1)} %get-tuple-element.14.partial, ...), custom_call_target="tpu_custom_call" | custom-call | tf_op jit(solution)/shard_map/coherence/pallas_call | solution.py:425

commit v5 on v4

--- a/solution.py
+++ b/solution.py
@@ -19,7 +19,7 @@
 
 
 def exchange_kernel(
-    dates, tiles, mine, above, rows, boxed, partial, partial_power, scale, own, core, below, relay, sums,
+    dates, tiles, mine, boxed, staged, above, rows, partial, partial_power, weights, band_out, own, core, below, relay, sums, scale,
     send, got_own, got_core, got_above, got_below, relay_send, relay_got, late_send, ready, late_ready,
 ):
     me = lax.axis_index("date")
@@ -69,42 +69,42 @@
         return is_near & (near_block == step) & is_first(0, tile + side)
 
     barrier = pltpu.get_barrier_semaphore()
-    count = jnp.int32(0)
+    from_first = is_first(near_block, tile)
+
+    @pl.when(~first)
+    def _():
+        for step, side in routes:
+            @when(there(side), me + step < dates)
+            def _():
+                signal(barrier, me + step, side)
+
+            @pl.when(around(step, side))
+            def _():
+                signal(barrier, dates + far_block - step, side)
+
+        for step, side in late:
+            @pl.when(to_first(step, side))
+            def _():
+                signal(barrier, 0, side)
+
+        @pl.when(from_first)
+        def _():
+            signal(barrier, 0)
+
+        @pl.when(starts)
+        def _():
+            signal(barrier, me + near)
+
+        @when(is_near, near_block < SHIFTS - 1)
+        def _():
+            signal(barrier, near_block + far)
+
+    count = first.astype(jnp.int32) + (is_near & ~from_first).astype(jnp.int32) + is_far.astype(jnp.int32)
     for step, side in routes:
-        @when(there(side), me + step < dates, ~first)
-        def _():
-            signal(barrier, me + step, side)
-
         count += straight(step, side).astype(jnp.int32)
         count += (there(side) & (me + step >= dates)).astype(jnp.int32)
-
-        @pl.when(around(step, side))
-        def _():
-            signal(barrier, dates + far_block - step, side)
-
     for step, side in late:
         count += (first & there(-side)).astype(jnp.int32)
-
-        @pl.when(to_first(step, side))
-        def _():
-            signal(barrier, 0, side)
-
-    from_first = is_first(near_block, tile)
-    count += first.astype(jnp.int32)
-
-    @pl.when(from_first)
-    def _():
-        signal(barrier, 0)
-
-    @when(starts, ~first)
-    def _():
-        signal(barrier, me + near)
-
-    @when(is_near, near_block < SHIFTS - 1)
-    def _():
-        signal(barrier, near_block + far)
-
-    count += (is_near & ~from_first).astype(jnp.int32) + is_far.astype(jnp.int32)
     pl.semaphore_wait(barrier, count)
 
     for step, side in routes:
@@ -173,6 +173,7 @@
     keep.wait()
 
     band = band_table(breadth)
+    band_out[...] = band
     total = height + 2 * row_reach
     above_rows = above.reshape(SHIFTS, 2, block * EDGE, breadth)
     below_rows = below.reshape(SHIFTS, 2, block * EDGE, breadth)
@@ -200,26 +201,39 @@
 
     for step in range(SHIFTS):
         squares = {row: square(rows, step, row) for row in range(row_reach if step == 0 else 0, total)}
+        upper = inner_sums(squares, EDGE) if step == 0 else window_sums(squares, 0, EDGE)
+        upper = jnp.concatenate(upper, axis=0)
         if step == 0:
-            store(inner_sums(squares, EDGE), partial_power)
-        else:
-            store(window_sums(squares, 0, EDGE), sums.at[0])
-            scale[step, 0] = lax.rsqrt(box_columns(by_date(sums.at[0], block), band)).reshape(block, EDGE, breadth)
-        store(window_sums(squares, EDGE, height), sums.at[1])
-        scale[step, 1] = lax.rsqrt(box_columns(by_date(sums.at[1], block), band)).reshape(block, EDGE, breadth)
+            partial_power[...] = upper
+        weights[step] = lax.rsqrt(box_columns(upper, band))
+        store(window_sums(squares, EDGE, height), sums.at[0])
+        scale[step] = lax.rsqrt(box_columns(by_date(sums.at[0], block), band)).reshape(block, EDGE, breadth)
+
+    inner = slice(row_reach * block, EDGE * block)
+    staged_rows = staged.reshape(SHIFTS, 2, block, block * EDGE, breadth)
 
     @pl.loop(0, SHIFTS)
     def _(step):
+        upper = []
         for date in range(block):
             real, imag = products(rows, rows, step, date, range(row_reach, total))
             for part, values in enumerate((real, imag)):
-                store(inner_sums(values, EDGE), partial.at[step, date, part])
+                found = inner_sums(values, EDGE)
+                store(found[:row_reach], partial.at[step, date, part])
+                upper += found[row_reach:]
                 store(window_sums(values, EDGE, height), sums.at[date * 2 + part])
+        columns = box_columns(jnp.concatenate(upper, axis=0), band)
         for date in range(block):
-            weight = scale[0, 1, date][None] * scale[step, 1]
+            for row in range(row_reach, EDGE):
+                weight = date_weight(weights, weights.at[step], row, date, block)
+                for part in range(2):
+                    at = ((date * 2 + part) * (EDGE - row_reach) + row - row_reach) * block
+                    staged_rows[step, part, date, pl.ds(row, block, stride=EDGE), :] = columns[at:at + block] * weight
+        for date in range(block):
+            weight = scale[0, date][None] * scale[step]
             for part in range(2):
                 columns = box_columns(by_date(sums.at[date * 2 + part], block), band)
-                boxed[part, step, date] = columns.reshape(block, EDGE, breadth) * weight
+                boxed[step, part, date] = columns.reshape(block, EDGE, breadth) * weight
 
     @when(starts, ~first)
     def _():
@@ -243,10 +257,6 @@
     def _():
         pl.semaphore_wait(ready, 1)
         to_relay(relay, near_block + far).start()
-
-    @pl.when(there(-1))
-    def _():
-        copy(0, 1, mine, me, send).wait_recv()
 
     for step, side in routes:
         @pl.when(straight(step, side))
@@ -267,30 +277,38 @@
     def _():
         to_relay(mine, me).wait_send()
 
+    @pl.when(there(-1))
+    def _():
+        copy(0, 1, mine, me, send).wait_recv()
+
 
 def exchange(acquired, dates, tiles):
     parts, block, height, breadth = acquired.shape
     total = height + 2 * row_reach
     edge = (SHIFTS, parts, block, EDGE, breadth)
+    tile = (SHIFTS, 2, block, block, EDGE, breadth)
     results = (
+        tile,
+        tile,
         edge,
         (SHIFTS, parts, total, block, breadth),
-        (2, SHIFTS, block, block, EDGE, breadth),
-        (SHIFTS, block, 2, EDGE * block, breadth),
+        (SHIFTS, block, 2, row_reach * block, breadth),
         (EDGE * block, breadth),
-        (SHIFTS, 2, block, EDGE, breadth),
+        (SHIFTS, EDGE * block, breadth),
     )
     return pl.pallas_call(
         functools.partial(exchange_kernel, dates, tiles),
-        out_shape=tuple(jax.ShapeDtypeStruct(shape, jnp.float32) for shape in results),
+        out_shape=tuple(jax.ShapeDtypeStruct(shape, jnp.float32) for shape in results) + (
+            jax.ShapeDtypeStruct((2 * breadth, breadth), jnp.bfloat16),),
         in_specs=[pl.BlockSpec(memory_space=pltpu.HBM)],
-        out_specs=(pl.BlockSpec(memory_space=pltpu.VMEM),) * len(results),
+        out_specs=(pl.BlockSpec(memory_space=pltpu.VMEM),) * (len(results) + 1),
         scratch_shapes=[
             pltpu.VMEM(acquired.shape, jnp.float32),
             pltpu.VMEM((SHIFTS - 1,) + acquired.shape, jnp.float32),
             pltpu.VMEM(edge, jnp.float32),
             pltpu.VMEM(acquired.shape, jnp.float32),
             pltpu.VMEM((2 * block, EDGE * block, breadth), jnp.float32),
+            pltpu.VMEM((SHIFTS, block, EDGE, breadth), jnp.float32),
             pltpu.SemaphoreType.DMA((SHIFTS, 3)),
             pltpu.SemaphoreType.DMA,
             pltpu.SemaphoreType.DMA((SHIFTS - 1,)),
@@ -367,82 +385,105 @@
     return sums
 
 
+def date_weight(first, second, row, date, block):
+    return jnp.broadcast_to(first[0, pl.ds(row * block + date, 1), :], (block, second.shape[-1])) * second[pl.ds(row * block, block), :]
+
+
 def coherence_kernel(
-    above, rows, boxed, partial, partial_power, scale, out, top, sums, weights, staged, done, done_boxed,
+    boxed, staged_before, above, rows, partial, partial_power, weights, band, out, staged, top, found, done, done_boxed,
 ):
-    block, breadth = out.shape[2], out.shape[5]
-    finished = pltpu.make_async_copy(boxed, out.at[:, :, :, :, pl.ds(EDGE, EDGE), :], done_boxed)
-    finished.start()
-    band = band_table(breadth)
+    block, height, breadth = out.shape[3:]
+
+    def copy_boxed(step):
+        return pltpu.make_async_copy(
+            boxed.at[step], out.at[:, step, :, :, pl.ds(EDGE, height - EDGE), :], done_boxed.at[step])
+
+    for step in range(SHIFTS):
+        copy_boxed(step).start()
     which = range(row_reach)
     above = above.reshape(SHIFTS, 2, block * EDGE, breadth)
+    staged_rows = staged.reshape(SHIFTS, 2, block, block * EDGE, breadth)
 
     for part in range(2):
         for row in which:
             top[0, part, row] = above[0, part, pl.ds(EDGE - row_reach + row, block, stride=EDGE), :]
-            for step in range(1, SHIFTS):
-                top[step, part, row] = rows[step, part, row]
-
-    def add_top(values, inner, ref):
-        tail = None
-        for row in reversed(which):
-            tail = values[row] if tail is None else tail + values[row]
-            at = pl.ds(row * block, block)
-            ref[at, :] = inner[at, :] + tail
-        at = pl.ds(row_reach * block, (EDGE - row_reach) * block)
-        ref[at, :] = inner[at, :]
-
-    add_top({row: square(top, 0, row) for row in which}, partial_power, sums.at[0])
-    weights[0] = lax.rsqrt(box_columns(by_date(sums.at[0], block), band)).reshape(block, EDGE, breadth)
-    for step in range(1, SHIFTS):
-        weights[step] = scale[step, 0]
-
-    def copy_out(step):
+
+    def with_top(values, inner):
+        tails = [values[row_reach - 1]]
+        for row in reversed(which[:-1]):
+            tails.insert(0, tails[0] + values[row])
+        return [tails[row] + inner[row * block:(row + 1) * block, :] for row in which]
+
+    power = with_top({row: square(top, 0, row) for row in which}, partial_power)
+    power = box_columns(jnp.concatenate(power, axis=0), band[...])
+    size = block // 2
+
+    def copy_out(step, half):
+        dates = pl.ds(half * size, size)
         return pltpu.make_async_copy(
-            staged.at[step], out.at[:, step, :, :, pl.ds(0, EDGE), :], done.at[step])
-
-    @pl.loop(0, SHIFTS)
-    def _(step):
-        for date in range(block):
-            both = products(top, top, step, date, which)
+            staged.at[step, :, dates], out.at[:, step, dates, :, pl.ds(0, EDGE), :], done.at[step, half])
+
+    def begin(step, half):
+        upper = []
+        for date in range(half * size, (half + 1) * size):
+            both = products(top, rows if step else top, step, date, which)
             for part, values in enumerate(both):
-                add_top(values, partial.at[step, date, part], sums.at[date * 2 + part])
-        for date in range(block):
-            weight = weights[0, date][None] * weights[step]
-            for part in range(2):
-                columns = box_columns(by_date(sums.at[date * 2 + part], block), band)
-                staged[step, part, date] = columns.reshape(block, EDGE, breadth) * weight
-        copy_out(step).start()
-
-    @pl.loop(0, SHIFTS)
-    def _(step):
-        copy_out(step).wait()
-
-    finished.wait()
-
-
-def coherence(block, height, breadth, *values):
+                upper += with_top(values, partial.at[step, date, part])
+        return box_columns(jnp.concatenate(upper, axis=0), band[...])
+
+    def end(step, half, columns):
+        for date in range(size):
+            for row in which:
+                weight = date_weight(found, weights.at[step] if step else found.at[0], row, half * size + date, block)
+                for part in range(2):
+                    at = ((date * 2 + part) * row_reach + row) * block
+                    rows_of = pl.ds(row, block, stride=EDGE)
+                    staged_rows[step, part, half * size + date, rows_of, :] = columns[at:at + block] * weight
+        copy_out(step, half).start()
+
+    pieces = [(step, half) for step in range(SHIFTS) for half in range(2)]
+    begun = None
+    for piece in pieces:
+        columns = begin(*piece)
+        if begun is None:
+            found[0] = lax.rsqrt(power)
+        else:
+            end(*begun)
+        begun = (*piece, columns)
+    end(*begun)
+
+    for step in range(SHIFTS):
+        copy_boxed(step).wait()
+    for piece in pieces:
+        copy_out(*piece).wait()
+
+
+def coherence(height, boxed, staged, *values):
+    block, breadth = staged.shape[2], staged.shape[5]
+    vmem = pl.BlockSpec(memory_space=pltpu.VMEM)
     return pl.pallas_call(
         coherence_kernel,
-        out_shape=jax.ShapeDtypeStruct((2, SHIFTS, block, block, height, breadth), jnp.float32),
-        in_specs=[pl.BlockSpec(memory_space=pltpu.VMEM)] * len(values),
-        out_specs=pl.BlockSpec(memory_space=pl.ANY),
+        out_shape=(
+            pltpu.HBM((2, SHIFTS, block, block, height, breadth), jnp.float32),
+            jax.ShapeDtypeStruct(staged.shape, jnp.float32),
+        ),
+        in_specs=[vmem] * (len(values) + 2),
+        out_specs=(pl.BlockSpec(memory_space=pltpu.HBM), vmem),
         scratch_shapes=[
-            pltpu.VMEM((SHIFTS, 2, row_reach, block, breadth), jnp.float32),
-            pltpu.VMEM((2 * block, EDGE * block, breadth), jnp.float32),
-            pltpu.VMEM((SHIFTS, block, EDGE, breadth), jnp.float32),
-            pltpu.VMEM((SHIFTS, 2, block, block, EDGE, breadth), jnp.float32),
+            pltpu.VMEM((1, 2, row_reach, block, breadth), jnp.float32),
+            pltpu.VMEM((1, row_reach * block, breadth), jnp.float32),
+            pltpu.SemaphoreType.DMA((SHIFTS, 2)),
             pltpu.SemaphoreType.DMA((SHIFTS,)),
-            pltpu.SemaphoreType.DMA,
         ],
-        compiler_params=pltpu.CompilerParams(vmem_limit_bytes=16 << 20),
+        input_output_aliases={1: 1},
+        compiler_params=pltpu.CompilerParams(vmem_limit_bytes=4 << 20),
         name="coherence",
-    )(*values)
+    )(boxed, staged, *values)[0]
 
 
 def solution(mesh):
     def on_device(acquired):
-        return coherence(*acquired.shape[1:], *exchange(acquired, mesh.shape["date"], mesh.shape["tile"]))
+        return coherence(acquired.shape[2], *exchange(acquired, mesh.shape["date"], mesh.shape["tile"]))
 
     in_specs = (P(None, "date", ("groups", "tile"), None),)
     out_specs = P(None, None, "date", None, ("groups", "tile"), None)

time: 46.8 us -> 46.4 us (level)
  Pallas kernels: 46.7 us -> 46.2 us
where the time goes in v5:
time: 46.4 us; the launch traced here: 46.2 us
  Pallas kernels  46.2 us (100%)
    pallas_call x1, Pallas kernels, exchange(): pl.pallas_call(functools.partial(exchange_kernel, dates, tiles), out_shap...  44.1 us
    pallas_call x1, Pallas kernels, coherence(): pl.pallas_call(coherence_kernel, out_shape=(pltpu.HBM((2, SHIFTS, block,...  2.11 us

profile of v5, /device:TPU:66, one launch (start us, length us, event | category | flops | bytes accessed | tf_op | source)
XLA Modules:
  0.0 46.2 jit_solution(8602985461593973459)
XLA Ops:
  0.0 44.1 %exchange.1 = (f32[4,2,8,8,8,128]{5,4,3,2,1,0:T(8,128)S(1)}, f32[4,2,8,8,8,128]{5,4,3,2,1,0:T(8,128)S(1)}, f32[4,2,8,8,128]{4,3,2,1,0:T(8,128)S(1)}, f32[4,2,26,...) custom-call(f32[2,8,16,128]{3,2,1,0:T(8,128)} %mine.1), custom_call_target="tpu_custom_call" | custom-call | tf_op jit(solution)/shard_map/exchange/pallas_call | solution.py:299
  44.1 2.1 %coherence.1 = (f32[2,4,8,8,16,128]{5,4,3,2,1,0:T(8,128)}, f32[4,2,8,8,8,128]{5,4,3,2,1,0:T(8,128)S(1)}) custom-call(f32[4,2,8,8,8,128]{5,4,3,2,1,0:T(8,128)S(1)} %get-tuple-element.14.boxed, f32[4,2,8,8,8,128]{5,4,3,2,1,0:T(8,128)S(1)} %get-tuple-element.15.staged_before, ...), custom_call_target="tpu_custom_call", output_to_operand_aliasing={{1}: (1, {})} | custom-call | tf_op jit(solution)/shard_map/coherence/pallas_call | solution.py:464

commit v6 on v5

--- a/solution.py
+++ b/solution.py
@@ -49,8 +49,8 @@
         if side == 0:
             return source, core.at[step - 1], got_core.at[step - 1]
         if side == 1:
-            return source.at[:, :, pl.ds(height - EDGE, EDGE), :], above.at[step], got_above.at[step]
-        return source.at[:, :, pl.ds(0, EDGE), :], below.at[step], got_below.at[step]
+            return source.at[:, :, pl.ds(height - row_reach, row_reach), :], above.at[step, :, :, pl.ds(EDGE - row_reach, row_reach), :], got_above.at[step]
+        return source.at[:, :, pl.ds(0, row_reach), :], below.at[step, :, :, pl.ds(0, row_reach), :], got_below.at[step]
 
     def copy(step, side, source, date, sems):
         src, dst, got = piece(step, side, source)
@@ -99,13 +99,15 @@
         def _():
             signal(barrier, near_block + far)
 
-    count = first.astype(jnp.int32) + (is_near & ~from_first).astype(jnp.int32) + is_far.astype(jnp.int32)
-    for step, side in routes:
-        count += straight(step, side).astype(jnp.int32)
-        count += (there(side) & (me + step >= dates)).astype(jnp.int32)
-    for step, side in late:
-        count += (first & there(-side)).astype(jnp.int32)
-    pl.semaphore_wait(barrier, count)
+        count = (is_near & ~from_first).astype(jnp.int32) + is_far.astype(jnp.int32)
+        for step, side in routes:
+            count += straight(step, side).astype(jnp.int32)
+            count += (there(side) & (me + step >= dates)).astype(jnp.int32)
+        pl.semaphore_wait(barrier, count)
+
+    @pl.when(first)
+    def _():
+        pl.semaphore_wait(barrier, SHIFTS + (SHIFTS + 1 if tiles > 1 else 0))
 
     for step, side in routes:
         @pl.when(straight(step, side))

time: 46.4 us -> 46 us (level)
  no operation moved by 1% of the time
where the time goes in v6:
time: 46 us; the launch traced here: 45.9 us
  Pallas kernels  45.9 us (100%)
    pallas_call x1, Pallas kernels, exchange(): pl.pallas_call(functools.partial(exchange_kernel, dates, tiles), out_shap...  43.8 us
    pallas_call x1, Pallas kernels, coherence(): pl.pallas_call(coherence_kernel, out_shape=(pltpu.HBM((2, SHIFTS, block,...  2.11 us

profile of v6, /device:TPU:66, one launch (start us, length us, event | category | flops | bytes accessed | tf_op | source)
XLA Modules:
  0.0 45.9 jit_solution(7387628726007140566)
XLA Ops:
  0.0 43.8 %exchange.1 = (f32[4,2,8,8,8,128]{5,4,3,2,1,0:T(8,128)S(1)}, f32[4,2,8,8,8,128]{5,4,3,2,1,0:T(8,128)S(1)}, f32[4,2,8,8,128]{4,3,2,1,0:T(8,128)S(1)}, f32[4,2,26,...) custom-call(f32[2,8,16,128]{3,2,1,0:T(8,128)} %mine.1), custom_call_target="tpu_custom_call" | custom-call | tf_op jit(solution)/shard_map/exchange/pallas_call | solution.py:301
  43.8 2.1 %coherence.1 = (f32[2,4,8,8,16,128]{5,4,3,2,1,0:T(8,128)}, f32[4,2,8,8,8,128]{5,4,3,2,1,0:T(8,128)S(1)}) custom-call(f32[4,2,8,8,8,128]{5,4,3,2,1,0:T(8,128)S(1)} %get-tuple-element.14.boxed, f32[4,2,8,8,8,128]{5,4,3,2,1,0:T(8,128)S(1)} %get-tuple-element.15.staged_before, ...), custom_call_target="tpu_custom_call", output_to_operand_aliasing={{1}: (1, {})} | custom-call | tf_op jit(solution)/shard_map/coherence/pallas_call | solution.py:466

commit v7 on v6

--- a/solution.py
+++ b/solution.py
@@ -20,7 +20,7 @@
 
 def exchange_kernel(
     dates, tiles, mine, boxed, staged, above, rows, partial, partial_power, weights, band_out, own, core, below, relay, sums, scale,
-    send, got_own, got_core, got_above, got_below, relay_send, relay_got, late_send, ready, late_ready,
+    send, got_own, got_core, got_above, got_below, relay_got, ready, late_ready,
 ):
     me = lax.axis_index("date")
     tile = lax.axis_index("tile")
@@ -47,15 +47,19 @@
 
     def piece(step, side, source):
         if side == 0:
-            return source, core.at[step - 1], got_core.at[step - 1]
+            return source, core.at[step - 1], got_core
         if side == 1:
-            return source.at[:, :, pl.ds(height - row_reach, row_reach), :], above.at[step, :, :, pl.ds(EDGE - row_reach, row_reach), :], got_above.at[step]
-        return source.at[:, :, pl.ds(0, row_reach), :], below.at[step, :, :, pl.ds(0, row_reach), :], got_below.at[step]
-
-    def copy(step, side, source, date, sems):
+            src, dst = pl.ds(height - row_reach, row_reach), pl.ds(EDGE - row_reach, row_reach)
+            return source.at[:, :, src, :], above.at[step, :, :, dst, :], got_above.at[min(step, 1)]
+        return source.at[:, :, pl.ds(0, row_reach), :], below.at[step, :, :, pl.ds(0, row_reach), :], got_below
+
+    def arrived(ref, semaphore):
+        pltpu.make_async_copy(ref, ref, semaphore).wait()
+
+    def copy(step, side, source, date):
         src, dst, got = piece(step, side, source)
         return pltpu.make_async_remote_copy(
-            src_ref=src, dst_ref=dst, send_sem=sems.at[step, side + 1], recv_sem=got,
+            src_ref=src, dst_ref=dst, send_sem=send.at[step, side + 1], recv_sem=got,
             device_id={"date": date, "tile": tile + side}, device_id_type=MESH,
         )
 
@@ -112,7 +116,7 @@
     for step, side in routes:
         @pl.when(straight(step, side))
         def _():
-            copy(step, side, mine, me - step, send).start()
+            copy(step, side, mine, me - step).start()
 
     keep = pltpu.make_async_copy(mine, own, got_own)
     keep.start()
@@ -145,13 +149,18 @@
 
     def to_relay(source, date):
         return pltpu.make_async_remote_copy(
-            src_ref=source, dst_ref=relay, send_sem=relay_send.at[0, 1], recv_sem=relay_got,
+            src_ref=source, dst_ref=relay, send_sem=send.at[0, 1], recv_sem=relay_got,
             device_id={"date": date, "tile": tile}, device_id_type=MESH,
         )
 
     @pl.when(first)
     def _():
         to_relay(mine, near).start()
+
+    for step, side in routes:
+        @pl.when(straight(step, side))
+        def _():
+            copy(step, side, mine, me - step).wait_send()
 
     @pl.when(is_far)
     def _():
@@ -164,13 +173,17 @@
             if step:
                 @pl.when(around(step, side))
                 def _():
-                    copy(step, side, relay, dates + far_block - step, relay_send).start()
-
-    for step, side in reversed(routes):
-        if (step, side) != (0, 1):
-            @pl.when(there(-side))
-            def _():
-                copy(step, side, mine, me, send).wait_recv()
+                    copy(step, side, relay, dates + far_block - step).start()
+
+    arrived(core, got_core)
+
+    @pl.when(there(1))
+    def _():
+        arrived(below.at[:, :, :, pl.ds(0, row_reach), :], got_below)
+
+    @pl.when(there(-1))
+    def _():
+        arrived(above.at[pl.ds(1, SHIFTS - 1), :, :, pl.ds(EDGE - row_reach, row_reach), :], got_above.at[1])
 
     keep.wait()
 
@@ -247,7 +260,7 @@
         def _():
             to_relay(mine, me).wait_recv()
             pl.semaphore_wait(late_ready, 1)
-            copy(step, side, relay, 0, late_send).start()
+            copy(step, side, relay, 0).start()
 
     serves_first = functools.reduce(jnp.logical_or, [to_first(step, side) for step, side in late])
 
@@ -261,19 +274,15 @@
         to_relay(relay, near_block + far).start()
 
     for step, side in routes:
-        @pl.when(straight(step, side))
-        def _():
-            copy(step, side, mine, me - step, send).wait_send()
-
         if step:
             @pl.when(around(step, side))
             def _():
-                copy(step, side, relay, dates + far_block - step, relay_send).wait_send()
+                copy(step, side, relay, dates + far_block - step).wait_send()
 
     for step, side in late:
         @pl.when(to_first(step, side))
         def _():
-            copy(step, side, relay, 0, late_send).wait_send()
+            copy(step, side, relay, 0).wait_send()
 
     @pl.when(starts | (is_near & (near_block < SHIFTS - 1)))
     def _():
@@ -281,7 +290,7 @@
 
     @pl.when(there(-1))
     def _():
-        copy(0, 1, mine, me, send).wait_recv()
+        copy(0, 1, mine, me).wait_recv()
 
 
 def exchange(acquired, dates, tiles):
@@ -313,12 +322,10 @@
             pltpu.VMEM((SHIFTS, block, EDGE, breadth), jnp.float32),
             pltpu.SemaphoreType.DMA((SHIFTS, 3)),
             pltpu.SemaphoreType.DMA,
-            pltpu.SemaphoreType.DMA((SHIFTS - 1,)),
-            pltpu.SemaphoreType.DMA((SHIFTS,)),
-            pltpu.SemaphoreType.DMA((SHIFTS,)),
-            pltpu.SemaphoreType.DMA((SHIFTS, 3)),
             pltpu.SemaphoreType.DMA,
-            pltpu.SemaphoreType.DMA((SHIFTS, 3)),
+            pltpu.SemaphoreType.DMA((2,)),
+            pltpu.SemaphoreType.DMA,
+            pltpu.SemaphoreType.DMA,
             pltpu.SemaphoreType.REGULAR,
             pltpu.SemaphoreType.REGULAR,
         ],
@@ -392,13 +399,13 @@
 
 
 def coherence_kernel(
-    boxed, staged_before, above, rows, partial, partial_power, weights, band, out, staged, top, found, done, done_boxed,
+    boxed, staged_before, above, rows, partial, partial_power, weights, band, out, staged, top, found, done,
 ):
     block, height, breadth = out.shape[3:]
 
     def copy_boxed(step):
         return pltpu.make_async_copy(
-            boxed.at[step], out.at[:, step, :, :, pl.ds(EDGE, height - EDGE), :], done_boxed.at[step])
+            boxed.at[step], out.at[:, step, :, :, pl.ds(EDGE, height - EDGE), :], done)
 
     for step in range(SHIFTS):
         copy_boxed(step).start()
@@ -423,7 +430,7 @@
     def copy_out(step, half):
         dates = pl.ds(half * size, size)
         return pltpu.make_async_copy(
-            staged.at[step, :, dates], out.at[:, step, dates, :, pl.ds(0, EDGE), :], done.at[step, half])
+            staged.at[step, :, dates], out.at[:, step, dates, :, pl.ds(0, EDGE), :], done)
 
     def begin(step, half):
         upper = []
@@ -454,10 +461,7 @@
         begun = (*piece, columns)
     end(*begun)
 
-    for step in range(SHIFTS):
-        copy_boxed(step).wait()
-    for piece in pieces:
-        copy_out(*piece).wait()
+    pltpu.make_async_copy(out, out, done).wait()
 
 
 def coherence(height, boxed, staged, *values):
@@ -474,8 +478,7 @@
         scratch_shapes=[
             pltpu.VMEM((1, 2, row_reach, block, breadth), jnp.float32),
             pltpu.VMEM((1, row_reach * block, breadth), jnp.float32),
-            pltpu.SemaphoreType.DMA((SHIFTS, 2)),
-            pltpu.SemaphoreType.DMA((SHIFTS,)),
+            pltpu.SemaphoreType.DMA,
         ],
         input_output_aliases={1: 1},
         compiler_params=pltpu.CompilerParams(vmem_limit_bytes=4 << 20),

time: 46 us -> 45.7 us (level)
  no operation moved by 1% of the time
where the time goes in v7:
time: 45.7 us; the launch traced here: 45.5 us
  Pallas kernels  45.5 us (100%)
    pallas_call x1, Pallas kernels, exchange(): pl.pallas_call(functools.partial(exchange_kernel, dates, tiles), out_shap...  43.5 us
    pallas_call x1, Pallas kernels, coherence(): pl.pallas_call(coherence_kernel, out_shape=(pltpu.HBM((2, SHIFTS, block,...  2.01 us

profile of v7, /device:TPU:66, one launch (start us, length us, event | category | flops | bytes accessed | tf_op | source)
XLA Modules:
  0.0 45.5 jit_solution(2005987824700172217)
XLA Ops:
  0.0 43.5 %exchange.1 = (f32[4,2,8,8,8,128]{5,4,3,2,1,0:T(8,128)S(1)}, f32[4,2,8,8,8,128]{5,4,3,2,1,0:T(8,128)S(1)}, f32[4,2,8,8,128]{4,3,2,1,0:T(8,128)S(1)}, f32[4,2,26,...) custom-call(f32[2,8,16,128]{3,2,1,0:T(8,128)} %mine.1), custom_call_target="tpu_custom_call" | custom-call | tf_op jit(solution)/shard_map/exchange/pallas_call | solution.py:310
  43.5 2.0 %coherence.1 = (f32[2,4,8,8,16,128]{5,4,3,2,1,0:T(8,128)}, f32[4,2,8,8,8,128]{5,4,3,2,1,0:T(8,128)S(1)}) custom-call(f32[4,2,8,8,8,128]{5,4,3,2,1,0:T(8,128)S(1)} %get-tuple-element.14.boxed, f32[4,2,8,8,8,128]{5,4,3,2,1,0:T(8,128)S(1)} %get-tuple-element.15.staged_before, ...), custom_call_target="tpu_custom_call", output_to_operand_aliasing={{1}: (1, {})} | custom-call | tf_op jit(solution)/shard_map/coherence/pallas_call | solution.py:470

commit v8 on v7

--- a/solution.py
+++ b/solution.py
@@ -59,7 +59,7 @@
     def copy(step, side, source, date):
         src, dst, got = piece(step, side, source)
         return pltpu.make_async_remote_copy(
-            src_ref=src, dst_ref=dst, send_sem=send.at[step, side + 1], recv_sem=got,
+            src_ref=src, dst_ref=dst, send_sem=send.at[side % 4], recv_sem=got,
             device_id={"date": date, "tile": tile + side}, device_id_type=MESH,
         )
 
@@ -113,10 +113,17 @@
     def _():
         pl.semaphore_wait(barrier, SHIFTS + (SHIFTS + 1 if tiles > 1 else 0))
 
-    for step, side in routes:
-        @pl.when(straight(step, side))
-        def _():
-            copy(step, side, mine, me - step).start()
+    for step in range(SHIFTS):
+        sides = [side for at, side in routes if at == step]
+        for side in sides:
+            @pl.when(straight(step, side))
+            def _():
+                copy(step, side, mine, me - step).start()
+
+        for side in sides:
+            @when(straight(step, side), starts)
+            def _():
+                copy(step, side, mine, me - step).wait_send()
 
     keep = pltpu.make_async_copy(mine, own, got_own)
     keep.start()
@@ -149,7 +156,7 @@
 
     def to_relay(source, date):
         return pltpu.make_async_remote_copy(
-            src_ref=source, dst_ref=relay, send_sem=send.at[0, 1], recv_sem=relay_got,
+            src_ref=source, dst_ref=relay, send_sem=send.at[2], recv_sem=relay_got,
             device_id={"date": date, "tile": tile}, device_id_type=MESH,
         )
 
@@ -157,10 +164,11 @@
     def _():
         to_relay(mine, near).start()
 
-    for step, side in routes:
-        @pl.when(straight(step, side))
-        def _():
-            copy(step, side, mine, me - step).wait_send()
+    edges = above.at[:, :, :, pl.ds(EDGE - row_reach, row_reach), :]
+    for side, sent in ((1, edges), (-1, edges), (0, core)):
+        @when(~starts, there(side))
+        def _():
+            arrived(sent, send.at[side % 4])
 
     @pl.when(is_far)
     def _():
@@ -169,11 +177,16 @@
         for step, side in routes:
             count += around(step, side).astype(jnp.int32)
         pl.semaphore_wait(ready, count)
-        for step, side in routes:
-            if step:
+        for step in range(1, SHIFTS):
+            for side in (1, -1, 0):
                 @pl.when(around(step, side))
                 def _():
                     copy(step, side, relay, dates + far_block - step).start()
+
+            for side in (1, -1, 0):
+                @pl.when(around(step, side))
+                def _():
+                    copy(step, side, relay, dates + far_block - step).wait_send()
 
     arrived(core, got_core)
 
@@ -272,12 +285,6 @@
     def _():
         pl.semaphore_wait(ready, 1)
         to_relay(relay, near_block + far).start()
-
-    for step, side in routes:
-        if step:
-            @pl.when(around(step, side))
-            def _():
-                copy(step, side, relay, dates + far_block - step).wait_send()
 
     for step, side in late:
         @pl.when(to_first(step, side))
@@ -320,7 +327,7 @@
             pltpu.VMEM(acquired.shape, jnp.float32),
             pltpu.VMEM((2 * block, EDGE * block, breadth), jnp.float32),
             pltpu.VMEM((SHIFTS, block, EDGE, breadth), jnp.float32),
-            pltpu.SemaphoreType.DMA((SHIFTS, 3)),
+            pltpu.SemaphoreType.DMA((4,)),
             pltpu.SemaphoreType.DMA,
             pltpu.SemaphoreType.DMA,
             pltpu.SemaphoreType.DMA((2,)),

time: 45.7 us -> 45.6 us (level)
  no operation moved by 1% of the time
where the time goes in v8:
time: 45.6 us; the launch traced here: 45.5 us
  Pallas kernels  45.5 us (100%)
    pallas_call x1, Pallas kernels, exchange(): pl.pallas_call(functools.partial(exchange_kernel, dates, tiles), out_shap...  43.4 us
    pallas_call x1, Pallas kernels, coherence(): pl.pallas_call(coherence_kernel, out_shape=(pltpu.HBM((2, SHIFTS, block,...  2.01 us

profile of v8, /device:TPU:66, one launch (start us, length us, event | category | flops | bytes accessed | tf_op | source)
XLA Modules:
  0.0 45.5 jit_solution(13344699264848998611)
XLA Ops:
  0.0 43.4 %exchange.1 = (f32[4,2,8,8,8,128]{5,4,3,2,1,0:T(8,128)S(1)}, f32[4,2,8,8,8,128]{5,4,3,2,1,0:T(8,128)S(1)}, f32[4,2,8,8,128]{4,3,2,1,0:T(8,128)S(1)}, f32[4,2,26,...) custom-call(f32[2,8,16,128]{3,2,1,0:T(8,128)} %mine.1), custom_call_target="tpu_custom_call" | custom-call | tf_op jit(solution)/shard_map/exchange/pallas_call | solution.py:317
  43.5 2.0 %coherence.1 = (f32[2,4,8,8,16,128]{5,4,3,2,1,0:T(8,128)}, f32[4,2,8,8,8,128]{5,4,3,2,1,0:T(8,128)S(1)}) custom-call(f32[4,2,8,8,8,128]{5,4,3,2,1,0:T(8,128)S(1)} %get-tuple-element.14.boxed, f32[4,2,8,8,8,128]{5,4,3,2,1,0:T(8,128)S(1)} %get-tuple-element.15.staged_before, ...), custom_call_target="tpu_custom_call", output_to_operand_aliasing={{1}: (1, {})} | custom-call | tf_op jit(solution)/shard_map/coherence/pallas_call | solution.py:477

commit v9 on v8

--- a/solution.py
+++ b/solution.py
@@ -19,8 +19,8 @@
 
 
 def exchange_kernel(
-    dates, tiles, mine, boxed, staged, above, rows, partial, partial_power, weights, band_out, own, core, below, relay, sums, scale,
-    send, got_own, got_core, got_above, got_below, relay_got, ready, late_ready,
+    dates, tiles, mine, boxed, staged, above, rows, partial, partial_power, weights, band_out, core, below, relay, sums, scale,
+    send, got_core, got_above, got_below, relay_got, ready,
 ):
     me = lax.axis_index("date")
     tile = lax.axis_index("tile")
@@ -47,7 +47,7 @@
 
     def piece(step, side, source):
         if side == 0:
-            return source, core.at[step - 1], got_core
+            return source, core.at[step], got_core
         if side == 1:
             src, dst = pl.ds(height - row_reach, row_reach), pl.ds(EDGE - row_reach, row_reach)
             return source.at[:, :, src, :], above.at[step, :, :, dst, :], got_above.at[min(step, 1)]
@@ -59,7 +59,7 @@
     def copy(step, side, source, date):
         src, dst, got = piece(step, side, source)
         return pltpu.make_async_remote_copy(
-            src_ref=src, dst_ref=dst, send_sem=send.at[side % 4], recv_sem=got,
+            src_ref=src, dst_ref=dst, send_sem=send.at[side % 3], recv_sem=got,
             device_id={"date": date, "tile": tile + side}, device_id_type=MESH,
         )
 
@@ -125,8 +125,7 @@
             def _():
                 copy(step, side, mine, me - step).wait_send()
 
-    keep = pltpu.make_async_copy(mine, own, got_own)
-    keep.start()
+    pltpu.make_async_copy(mine, core.at[0], got_core).start()
 
     @when(is_near, ~from_first)
     def _():
@@ -144,7 +143,7 @@
     for step, side in late:
         @when(first, there(-side))
         def _():
-            signal(late_ready, step + near, -side)
+            signal(ready, step + near, -side)
 
     @pl.when(tile == 0)
     def _():
@@ -156,7 +155,7 @@
 
     def to_relay(source, date):
         return pltpu.make_async_remote_copy(
-            src_ref=source, dst_ref=relay, send_sem=send.at[2], recv_sem=relay_got,
+            src_ref=source, dst_ref=relay, send_sem=send.at[1], recv_sem=relay_got,
             device_id={"date": date, "tile": tile}, device_id_type=MESH,
         )
 
@@ -165,10 +164,10 @@
         to_relay(mine, near).start()
 
     edges = above.at[:, :, :, pl.ds(EDGE - row_reach, row_reach), :]
-    for side, sent in ((1, edges), (-1, edges), (0, core)):
+    for side, sent in ((1, edges), (-1, edges), (0, core.at[pl.ds(1, SHIFTS - 1)])):
         @when(~starts, there(side))
         def _():
-            arrived(sent, send.at[side % 4])
+            arrived(sent, send.at[side % 3])
 
     @pl.when(is_far)
     def _():
@@ -198,15 +197,12 @@
     def _():
         arrived(above.at[pl.ds(1, SHIFTS - 1), :, :, pl.ds(EDGE - row_reach, row_reach), :], got_above.at[1])
 
-    keep.wait()
-
     band = band_table(breadth)
     band_out[...] = band
     total = height + 2 * row_reach
     above_rows = above.reshape(SHIFTS, 2, block * EDGE, breadth)
     below_rows = below.reshape(SHIFTS, 2, block * EDGE, breadth)
-    own_rows = own.reshape(2, block * height, breadth)
-    core_rows = core.reshape(SHIFTS - 1, 2, block * height, breadth)
+    core_rows = core.reshape(SHIFTS, 2, block * height, breadth)
 
     for step in range(SHIFTS):
         for part in range(2):
@@ -219,9 +215,8 @@
     for row in range(height):
         for part in range(2):
             at = pl.ds(row, block, stride=height)
-            rows[0, part, row_reach + row] = own_rows[part, at, :]
-            for step in range(1, SHIFTS):
-                rows[step, part, row_reach + row] = core_rows[step - 1, part, at, :]
+            for step in range(SHIFTS):
+                rows[step, part, row_reach + row] = core_rows[step, part, at, :]
 
     def store(values, ref):
         for row, value in enumerate(values):
@@ -268,22 +263,26 @@
         pl.semaphore_wait(ready, 1)
         to_relay(mine, me + near).start()
 
+    passes_on = is_near & (near_block < SHIFTS - 1)
+
+    @pl.when(is_near)
+    def _():
+        to_relay(mine, me).wait_recv()
+        count = passes_on.astype(jnp.int32)
+        for step, side in late:
+            count += to_first(step, side).astype(jnp.int32)
+
+        @pl.when(count > 0)
+        def _():
+            pl.semaphore_wait(ready, count)
+
     for step, side in late:
         @pl.when(to_first(step, side))
         def _():
-            to_relay(mine, me).wait_recv()
-            pl.semaphore_wait(late_ready, 1)
             copy(step, side, relay, 0).start()
 
-    serves_first = functools.reduce(jnp.logical_or, [to_first(step, side) for step, side in late])
-
-    @when(is_near, ~serves_first)
-    def _():
-        to_relay(mine, me).wait_recv()
-
-    @when(is_near, near_block < SHIFTS - 1)
-    def _():
-        pl.semaphore_wait(ready, 1)
+    @pl.when(passes_on)
+    def _():
         to_relay(relay, near_block + far).start()
 
     for step, side in late:
@@ -321,19 +320,16 @@
         in_specs=[pl.BlockSpec(memory_space=pltpu.HBM)],
         out_specs=(pl.BlockSpec(memory_space=pltpu.VMEM),) * (len(results) + 1),
         scratch_shapes=[
-            pltpu.VMEM(acquired.shape, jnp.float32),
-            pltpu.VMEM((SHIFTS - 1,) + acquired.shape, jnp.float32),
+            pltpu.VMEM((SHIFTS,) + acquired.shape, jnp.float32),
             pltpu.VMEM(edge, jnp.float32),
             pltpu.VMEM(acquired.shape, jnp.float32),
             pltpu.VMEM((2 * block, EDGE * block, breadth), jnp.float32),
             pltpu.VMEM((SHIFTS, block, EDGE, breadth), jnp.float32),
-            pltpu.SemaphoreType.DMA((4,)),
-            pltpu.SemaphoreType.DMA,
+            pltpu.SemaphoreType.DMA((3,)),
             pltpu.SemaphoreType.DMA,
             pltpu.SemaphoreType.DMA((2,)),
             pltpu.SemaphoreType.DMA,
             pltpu.SemaphoreType.DMA,
-            pltpu.SemaphoreType.REGULAR,
             pltpu.SemaphoreType.REGULAR,
         ],
         compiler_params=pltpu.CompilerParams(

time: 45.6 us -> 45.6 us (level)
  no operation moved by 1% of the time
where the time goes in v9:
time: 45.6 us; the launch traced here: 45.4 us
  Pallas kernels  45.4 us (100%)
    pallas_call x1, Pallas kernels, exchange(): pl.pallas_call(functools.partial(exchange_kernel, dates, tiles), out_shap...  43.4 us
    pallas_call x1, Pallas kernels, coherence(): pl.pallas_call(coherence_kernel, out_shape=(pltpu.HBM((2, SHIFTS, block,...  2.01 us

profile of v9, /device:TPU:66, one launch (start us, length us, event | category | flops | bytes accessed | tf_op | source)
XLA Modules:
  0.0 45.4 jit_solution(17433147620041565600)
XLA Ops:
  0.0 43.4 %exchange.1 = (f32[4,2,8,8,8,128]{5,4,3,2,1,0:T(8,128)S(1)}, f32[4,2,8,8,8,128]{5,4,3,2,1,0:T(8,128)S(1)}, f32[4,2,8,8,128]{4,3,2,1,0:T(8,128)S(1)}, f32[4,2,26,...) custom-call(f32[2,8,16,128]{3,2,1,0:T(8,128)} %mine.1), custom_call_target="tpu_custom_call" | custom-call | tf_op jit(solution)/shard_map/exchange/pallas_call | solution.py:316
  43.4 2.0 %coherence.1 = (f32[2,4,8,8,16,128]{5,4,3,2,1,0:T(8,128)}, f32[4,2,8,8,8,128]{5,4,3,2,1,0:T(8,128)S(1)}) custom-call(f32[4,2,8,8,8,128]{5,4,3,2,1,0:T(8,128)S(1)} %get-tuple-element.14.boxed, f32[4,2,8,8,8,128]{5,4,3,2,1,0:T(8,128)S(1)} %get-tuple-element.15.staged_before, ...), custom_call_target="tpu_custom_call", output_to_operand_aliasing={{1}: (1, {})} | custom-call | tf_op jit(solution)/shard_map/coherence/pallas_call | solution.py:473
